TPU v7x, 16 devices: a 4x2x1 block of a 4x4x8 slice. The times are simulated.
16 devices in a mesh: dp: 2 (over y, z), cp: 8 (over x, core).
Axes of the slice: x: 4, y: 2, z: 1, core: 2. Of those that a mesh axis runs over, the one named last changes fastest.
The devices are a block of a 4x4x8 slice.
Arguments:
- q_raw: bfloat16 [16384, 16, 128], P(('dp', 'cp')), parts along dimension 0
- k_raw: bfloat16 [16384, 8, 128], P(('dp', 'cp')), parts along dimension 0
- v_proj: bfloat16 [16384, 8, 128], P(('dp', 'cp')), parts along dimension 0
- out_fwd: bfloat16 [16384, 16, 128], P(('dp', 'cp')), parts along dimension 0
- lse_fwd: float32 [16384, 16], P(('dp', 'cp')), parts along dimension 0
- d_out: bfloat16 [16384, 16, 128], P(('dp', 'cp')), parts along dimension 0
- q_norm: float32 [128], replicated
- k_norm: float32 [128], replicated
Outputs:
- output 1: bfloat16 [16384, 16, 128], P(('dp', 'cp')), parts along dimension 0
- output 2: bfloat16 [16384, 8, 128], P(('dp', 'cp')), parts along dimension 0
- output 3: bfloat16 [16384, 8, 128], P(('dp', 'cp')), parts along dimension 0
- output 4: float32 [256], P('dp'), parts along dimension 0
- output 5: float32 [256], P('dp'), parts along dimension 0
There are 2 independent parts. A program takes and returns all parts, laid end to end along the dimension named above; an argument that names none is the same for every part.
All inputs are finite; a program needn't handle non-finite values.
Results may differ from a plain program's by a relative error of at most 0.00316113.
Values are sent between devices in bfloat16 or wider.
A program may use at most 768 MiB of HBM per device.

v0:
```python
import jax
import jax.numpy as jnp
from jax import lax
from jax.sharding import PartitionSpec as P

HEAD_DIM = 128
ROPE_THETA = 1000000.0
NORM_EPS = 1e-6


def rope_tables(positions):
    inv_freq = ROPE_THETA ** (-jnp.arange(0, HEAD_DIM, 2).astype(jnp.float32) / HEAD_DIM)
    angles = positions.astype(jnp.float32)[:, None] * inv_freq[None, :]
    angles = jnp.concatenate([angles, angles], axis=-1)
    return jnp.cos(angles)[:, None, :], jnp.sin(angles)[:, None, :]


def norm_rope(raw_in, weight, cos_t, sin_t):
    mean_sq = jnp.mean(raw_in * raw_in, axis=-1, keepdims=True)
    normed = raw_in * lax.rsqrt(mean_sq + NORM_EPS) * weight
    half_dim = raw_in.shape[-1] // 2
    rotated = jnp.concatenate([-normed[..., half_dim:], normed[..., :half_dim]], axis=-1)
    return normed * cos_t + rotated * sin_t


def pair_grads(q_blk, do_blk, lse_blk, delta_blk, k_blk, v_blk, visible):
    sm_scale = HEAD_DIM ** -0.5
    logits = jnp.einsum('qngd,knd->qngk', q_blk, k_blk, preferred_element_type=jnp.float32) * sm_scale - lse_blk[..., None]
    if visible is not None:
        logits = jnp.where(visible[:, None, None, :], logits, -jnp.inf)
    attn_prob = jnp.exp(logits)
    attn_dprob = jnp.einsum('qngd,knd->qngk', do_blk, v_blk, preferred_element_type=jnp.float32)
    score_grad = (attn_prob * (attn_dprob - delta_blk[..., None])).astype(jnp.bfloat16)
    prob_bf = attn_prob.astype(jnp.bfloat16)
    dq_part = sm_scale * jnp.einsum('qngk,knd->qngd', score_grad, k_blk, preferred_element_type=jnp.float32)
    dk_part = sm_scale * jnp.einsum('qngk,qngd->knd', score_grad, q_blk, preferred_element_type=jnp.float32)
    dv_part = jnp.einsum('qngk,qngd->knd', prob_bf, do_blk, preferred_element_type=jnp.float32)
    return dq_part, dk_part, dv_part


def own_grads(q_b, do_b, lse_b, delta_sum, k_blk, v_blk):
    chunk_len = k_blk.shape[0] // 2
    tri_mask = jnp.arange(chunk_len)[:, None] >= jnp.arange(chunk_len)[None, :]
    dq_first, dk_first, dv_first = pair_grads(q_b[:chunk_len], do_b[:chunk_len], lse_b[:chunk_len], delta_sum[:chunk_len], k_blk[:chunk_len], v_blk[:chunk_len], tri_mask)
    dq_cross, dk_cross, dv_cross = pair_grads(q_b[chunk_len:], do_b[chunk_len:], lse_b[chunk_len:], delta_sum[chunk_len:], k_blk[:chunk_len], v_blk[:chunk_len], None)
    dq_second, dk_second, dv_second = pair_grads(q_b[chunk_len:], do_b[chunk_len:], lse_b[chunk_len:], delta_sum[chunk_len:], k_blk[chunk_len:], v_blk[chunk_len:], tri_mask)
    dq_own = jnp.concatenate([dq_first, dq_cross + dq_second])
    dk_own = jnp.concatenate([dk_first + dk_cross, dk_second])
    dv_own = jnp.concatenate([dv_first + dv_cross, dv_second])
    return dq_own, dk_own, dv_own


def early_source(q_b, do_b, lse_b, delta_sum, k_blk, v_blk, dq_acc, dk_acc, dv_acc):
    chunk_len = k_blk.shape[0] // 2
    dq_part, dk_part, dv_part = pair_grads(q_b, do_b, lse_b, delta_sum, k_blk[:chunk_len], v_blk[:chunk_len], None)
    return (dq_acc + dq_part,
            jnp.concatenate([dk_acc[:chunk_len] + dk_part, dk_acc[chunk_len:]]),
            jnp.concatenate([dv_acc[:chunk_len] + dv_part, dv_acc[chunk_len:]]))


def late_source(q_b, do_b, lse_b, delta_sum, k_blk, v_blk, dq_acc, dk_acc, dv_acc):
    chunk_len = k_blk.shape[0] // 2
    dq_part, dk_part, dv_part = pair_grads(q_b[chunk_len:], do_b[chunk_len:], lse_b[chunk_len:], delta_sum[chunk_len:], k_blk, v_blk, None)
    return (jnp.concatenate([dq_acc[:chunk_len], dq_acc[chunk_len:] + dq_part]),
            dk_acc + dk_part,
            dv_acc + dv_part)


def solution(mesh):
    cp_size = mesh.shape['cp']
    shift_pairs = [(source, (source + 1) % cp_size) for source in range(cp_size)]

    def local_grads(q_raw, k_raw, v_proj, out_fwd, lse_fwd, d_out, q_norm, k_norm):
        dev_rank = lax.axis_index('cp')
        local_rows, num_heads = q_raw.shape[0], q_raw.shape[1]
        chunk_len = local_rows // 2
        kv_heads = k_raw.shape[1]
        per_kv = num_heads // kv_heads
        offsets = jnp.arange(chunk_len)
        positions = jnp.concatenate([dev_rank * chunk_len + offsets, (2 * cp_size - 1 - dev_rank) * chunk_len + offsets])
        cos_t, sin_t = rope_tables(positions)
        prepare = lambda raw_in, weight: norm_rope(raw_in, weight, cos_t, sin_t)
        q_full, pull_q = jax.vjp(prepare, q_raw.astype(jnp.float32), q_norm)
        k_full, pull_k = jax.vjp(prepare, k_raw.astype(jnp.float32), k_norm)
        q_b = q_full.astype(jnp.bfloat16).reshape(local_rows, kv_heads, per_kv, HEAD_DIM)
        k_b = k_full.astype(jnp.bfloat16)
        do_b = d_out.reshape(local_rows, kv_heads, per_kv, HEAD_DIM)
        lse_b = lse_fwd.reshape(local_rows, kv_heads, per_kv)
        delta_sum = jnp.einsum('thd,thd->th', d_out, out_fwd, preferred_element_type=jnp.float32).reshape(local_rows, kv_heads, per_kv)
        dq_acc, dk_acc, dv_acc = own_grads(q_b, do_b, lse_b, delta_sum, k_b, v_proj)

        def visit_source(step_idx, loop_state):
            k_cur, v_cur, dq_cur, dk_cur, dv_cur = loop_state
            k_cur = lax.ppermute(k_cur, 'cp', shift_pairs)
            v_cur = lax.ppermute(v_cur, 'cp', shift_pairs)
            dk_cur = lax.ppermute(dk_cur, 'cp', shift_pairs)
            dv_cur = lax.ppermute(dv_cur, 'cp', shift_pairs)
            source = (dev_rank - step_idx) % cp_size
            dq_cur, dk_cur, dv_cur = lax.cond(source < dev_rank, early_source, late_source, q_b, do_b, lse_b, delta_sum, k_cur, v_cur, dq_cur, dk_cur, dv_cur)
            return k_cur, v_cur, dq_cur, dk_cur, dv_cur

        loop_state = lax.fori_loop(1, cp_size, visit_source, (k_b, v_proj, dq_acc, dk_acc, dv_acc))
        dq_acc, dk_cur, dv_cur = loop_state[2], loop_state[3], loop_state[4]
        dk_home = lax.ppermute(dk_cur, 'cp', shift_pairs)
        dv_home = lax.ppermute(dv_cur, 'cp', shift_pairs)
        dq_raw, dq_weight = pull_q(dq_acc.reshape(local_rows, num_heads, HEAD_DIM))
        dk_raw, dk_weight = pull_k(dk_home)
        return (dq_raw.astype(jnp.bfloat16), dk_raw.astype(jnp.bfloat16), dv_home.astype(jnp.bfloat16),
                lax.psum(dq_weight, 'cp'), lax.psum(dk_weight, 'cp'))

    row_spec = P(('dp', 'cp'))
    in_specs = (row_spec, row_spec, row_spec, row_spec, row_spec, row_spec, P(), P())
    out_specs = (row_spec, row_spec, row_spec, P('dp'), P('dp'))
    return jax.shard_map(local_grads, mesh=mesh, in_specs=in_specs, out_specs=out_specs, check_vma=False)
```

profile of v0, /device:TPU:113, one launch (start us, length us, event | category | flops | bytes accessed | tf_op | source)
XLA Modules:
  0.0 2010.7 jit_solution(7637374754374743788)
XLA Ops:
  42.1 10.4 fusion.63
  91.8 10.7 fusion.87
  102.4 10.8 fusion.41
  174.0 12.7 fusion.81
  224.2 1662.1 %while.23 = (s32[]{:T(128)}, bf16[1024,8,128]{2,0,1:T(8,128)(2,1)}, bf16[1024,8,128]{2,0,1:T(8,128)(2,1)}, f32[1024,8,2,128]{3,0,2,1:T(8,128)}, f32[1024,8,128]{...) while((s32[]{:T(128)}, bf16[1024,8,128]{2,0,1:T(8,128)(2,1)}, ...), condition=%wide.region_5.6_spmd, body=%wide.region_2.5_spmd.sunk | while | flops 10812391424 | bytes 291734144 | solution.py:102
  252.2 111.0 %collective-permute-done.1 = bf16[1024,8,128]{2,0,1:T(8,128)(2,1)} collective-permute-done((bf16[1024,8,128]{2,0,1:T(8,128)(2,1)}, bf16[1024,8,128]{2,0,1:T(8,128)(2,1)}, u32[]{:S(2)}, u32[]{:S(2)}) %collective-permute-start.1) | collective-permute-done | bytes 2097184 | tf_op jit(solution)/shard_map/while/body/eval_jaxpr/ppermute | solution.py:95
  366.3 19.4 collective-permute-done
  387.1 97.6 %conditional.2 = (f32[1024,8,2,128]{3,0,2,1:T(8,128)}, f32[1024,8,128]{2,0,1:T(8,128)}, f32[1024,8,128]{2,0,1:T(8,128)}) conditional(s32[]{:T(128)} %convert_element_type.156, (f32[1024,8,2,128]{3,0,2,1:T(8,128)}, bf16[1024,8,2,128]{3,0,2,1:T(8,128)(2,1)}, bf16[1024,8,128]{2,0,1:T(8,128)(2,1)S(1)}, f32[1024,8,2]{0,2,1:T(2,128)S(1)}, ...), branch_computations={%region_3.3_spmd, %region_4.4_spmd} | conditional | flops 10812391424 | bytes 233013312 | solution.py:99
  393.4 17.8 fusion.34
  411.2 16.9 bitcast_add_fusion.4
  428.1 22.3 %fusion.23 = bf16[1024,8,2,512]{0,3,2,1:T(8,128)(2,1)} fusion(f32[8,512,1024,2]{2,1,3,0:T(8,128)} %fusion.34, f32[1024,8,2]{0,2,1:T(2,128)S(1)} %sub.28, f32[1024,8,2]{0,2,1:T(2,128)S(1)} %sub.25, bf16[1024,8,2,128]{3,0,2,1:T(8,128)(2,1)} %get-tuple-element.359, bf16[1024,8,128]{2,0,1:T(8,128)(2,1)} %get-tuple-element.358), kind=kOutput, calls=%fused_computation.26 | convolution fusion | flops 2189426688 | bytes 55705600 | tf_op jit(solution)/shard_map/while/body/eval_jaxpr/cond/branch_1_fun/qngd,knd->qngk/dot_general | solution.py:32
  450.3 13.4 bitcast_add_fusion.5
  463.7 13.2 bitcast_add_fusion.3
  488.9 111.1 %collective-permute-done.1 = bf16[1024,8,128]{2,0,1:T(8,128)(2,1)} collective-permute-done((bf16[1024,8,128]{2,0,1:T(8,128)(2,1)}, bf16[1024,8,128]{2,0,1:T(8,128)(2,1)}, u32[]{:S(2)}, u32[]{:S(2)}) %collective-permute-start.1) | collective-permute-done | bytes 2097184 | tf_op jit(solution)/shard_map/while/body/eval_jaxpr/ppermute | solution.py:95
  603.0 19.4 collective-permute-done
  623.8 92.3 %conditional.2 = (f32[1024,8,2,128]{3,0,2,1:T(8,128)}, f32[1024,8,128]{2,0,1:T(8,128)}, f32[1024,8,128]{2,0,1:T(8,128)}) conditional(s32[]{:T(128)} %convert_element_type.156, (f32[1024,8,2,128]{3,0,2,1:T(8,128)}, bf16[1024,8,2,128]{3,0,2,1:T(8,128)(2,1)}, bf16[1024,8,128]{2,0,1:T(8,128)(2,1)S(1)}, f32[1024,8,2]{0,2,1:T(2,128)S(1)}, ...), branch_computations={%region_3.3_spmd, %region_4.4_spmd} | conditional | flops 10812391424 | bytes 233013312 | solution.py:99
  628.4 17.2 fusion.13
  645.6 17.3 bitcast_add_fusion
  662.9 21.6 %fusion.1 = bf16[512,8,2,1024]{0,3,2,1:T(8,128)(2,1)} fusion(f32[8,1024,512,2]{2,1,3,0:T(8,128)} %fusion.13, f32[512,8,2]{0,2,1:T(2,128)S(1)} %slice.79, f32[512,8,2]{0,2,1:T(2,128)S(1)} %slice.77, bf16[1024,8,128]{2,0,1:T(8,128)(2,1)} %get-tuple-element.349, bf16[1024,8,2,128]{3,0,2,1:T(8,128)(2,1)} %get-tuple-element.350), kind=kOutput, calls=%fused_computation.2 | convolution fusion | flops 2189426688 | bytes 54591488 | tf_op jit(solution)/shard_map/while/body/eval_jaxpr/cond/branch_0_fun/qngd,knd->qngk/dot_general | solution.py:32
  684.5 14.0 bitcast_add_fusion.1
  698.6 11.4 bitcast_add_fusion.2
  725.6 111.1 %collective-permute-done.1 = bf16[1024,8,128]{2,0,1:T(8,128)(2,1)} collective-permute-done((bf16[1024,8,128]{2,0,1:T(8,128)(2,1)}, bf16[1024,8,128]{2,0,1:T(8,128)(2,1)}, u32[]{:S(2)}, u32[]{:S(2)}) %collective-permute-start.1) | collective-permute-done | bytes 2097184 | tf_op jit(solution)/shard_map/while/body/eval_jaxpr/ppermute | solution.py:95
  839.7 19.4 collective-permute-done
  860.5 92.3 %conditional.2 = (f32[1024,8,2,128]{3,0,2,1:T(8,128)}, f32[1024,8,128]{2,0,1:T(8,128)}, f32[1024,8,128]{2,0,1:T(8,128)}) conditional(s32[]{:T(128)} %convert_element_type.156, (f32[1024,8,2,128]{3,0,2,1:T(8,128)}, bf16[1024,8,2,128]{3,0,2,1:T(8,128)(2,1)}, bf16[1024,8,128]{2,0,1:T(8,128)(2,1)S(1)}, f32[1024,8,2]{0,2,1:T(2,128)S(1)}, ...), branch_computations={%region_3.3_spmd, %region_4.4_spmd} | conditional | flops 10812391424 | bytes 233013312 | solution.py:99
  865.1 17.2 fusion.13
  882.3 17.3 bitcast_add_fusion
  899.6 21.6 %fusion.1 = bf16[512,8,2,1024]{0,3,2,1:T(8,128)(2,1)} fusion(f32[8,1024,512,2]{2,1,3,0:T(8,128)} %fusion.13, f32[512,8,2]{0,2,1:T(2,128)S(1)} %slice.79, f32[512,8,2]{0,2,1:T(2,128)S(1)} %slice.77, bf16[1024,8,128]{2,0,1:T(8,128)(2,1)} %get-tuple-element.349, bf16[1024,8,2,128]{3,0,2,1:T(8,128)(2,1)} %get-tuple-element.350), kind=kOutput, calls=%fused_computation.2 | convolution fusion | flops 2189426688 | bytes 54591488 | tf_op jit(solution)/shard_map/while/body/eval_jaxpr/cond/branch_0_fun/qngd,knd->qngk/dot_general | solution.py:32
  921.2 14.0 bitcast_add_fusion.1
  935.2 11.4 bitcast_add_fusion.2
  962.3 105.9 %collective-permute-done.1 = bf16[1024,8,128]{2,0,1:T(8,128)(2,1)} collective-permute-done((bf16[1024,8,128]{2,0,1:T(8,128)(2,1)}, bf16[1024,8,128]{2,0,1:T(8,128)(2,1)}, u32[]{:S(2)}, u32[]{:S(2)}) %collective-permute-start.1) | collective-permute-done | bytes 2097184 | tf_op jit(solution)/shard_map/while/body/eval_jaxpr/ppermute | solution.py:95
  1071.2 19.4 collective-permute-done
  1092.0 92.3 %conditional.2 = (f32[1024,8,2,128]{3,0,2,1:T(8,128)}, f32[1024,8,128]{2,0,1:T(8,128)}, f32[1024,8,128]{2,0,1:T(8,128)}) conditional(s32[]{:T(128)} %convert_element_type.156, (f32[1024,8,2,128]{3,0,2,1:T(8,128)}, bf16[1024,8,2,128]{3,0,2,1:T(8,128)(2,1)}, bf16[1024,8,128]{2,0,1:T(8,128)(2,1)S(1)}, f32[1024,8,2]{0,2,1:T(2,128)S(1)}, ...), branch_computations={%region_3.3_spmd, %region_4.4_spmd} | conditional | flops 10812391424 | bytes 233013312 | solution.py:99
  1096.7 17.2 fusion.13
  1113.8 17.3 bitcast_add_fusion
  1131.1 21.6 %fusion.1 = bf16[512,8,2,1024]{0,3,2,1:T(8,128)(2,1)} fusion(f32[8,1024,512,2]{2,1,3,0:T(8,128)} %fusion.13, f32[512,8,2]{0,2,1:T(2,128)S(1)} %slice.79, f32[512,8,2]{0,2,1:T(2,128)S(1)} %slice.77, bf16[1024,8,128]{2,0,1:T(8,128)(2,1)} %get-tuple-element.349, bf16[1024,8,2,128]{3,0,2,1:T(8,128)(2,1)} %get-tuple-element.350), kind=kOutput, calls=%fused_computation.2 | convolution fusion | flops 2189426688 | bytes 54591488 | tf_op jit(solution)/shard_map/while/body/eval_jaxpr/cond/branch_0_fun/qngd,knd->qngk/dot_general | solution.py:32
  1152.7 14.0 bitcast_add_fusion.1
  1166.8 11.4 bitcast_add_fusion.2
  1199.0 100.7 %collective-permute-done.1 = bf16[1024,8,128]{2,0,1:T(8,128)(2,1)} collective-permute-done((bf16[1024,8,128]{2,0,1:T(8,128)(2,1)}, bf16[1024,8,128]{2,0,1:T(8,128)(2,1)}, u32[]{:S(2)}, u32[]{:S(2)}) %collective-permute-start.1) | collective-permute-done | bytes 2097184 | tf_op jit(solution)/shard_map/while/body/eval_jaxpr/ppermute | solution.py:95
  1302.7 19.4 collective-permute-done
  1323.5 92.4 %conditional.2 = (f32[1024,8,2,128]{3,0,2,1:T(8,128)}, f32[1024,8,128]{2,0,1:T(8,128)}, f32[1024,8,128]{2,0,1:T(8,128)}) conditional(s32[]{:T(128)} %convert_element_type.156, (f32[1024,8,2,128]{3,0,2,1:T(8,128)}, bf16[1024,8,2,128]{3,0,2,1:T(8,128)(2,1)}, bf16[1024,8,128]{2,0,1:T(8,128)(2,1)S(1)}, f32[1024,8,2]{0,2,1:T(2,128)S(1)}, ...), branch_computations={%region_3.3_spmd, %region_4.4_spmd} | conditional | flops 10812391424 | bytes 233013312 | solution.py:99
  1328.2 17.2 fusion.13
  1345.3 17.3 bitcast_add_fusion
  1362.6 21.6 %fusion.1 = bf16[512,8,2,1024]{0,3,2,1:T(8,128)(2,1)} fusion(f32[8,1024,512,2]{2,1,3,0:T(8,128)} %fusion.13, f32[512,8,2]{0,2,1:T(2,128)S(1)} %slice.79, f32[512,8,2]{0,2,1:T(2,128)S(1)} %slice.77, bf16[1024,8,128]{2,0,1:T(8,128)(2,1)} %get-tuple-element.349, bf16[1024,8,2,128]{3,0,2,1:T(8,128)(2,1)} %get-tuple-element.350), kind=kOutput, calls=%fused_computation.2 | convolution fusion | flops 2189426688 | bytes 54591488 | tf_op jit(solution)/shard_map/while/body/eval_jaxpr/cond/branch_0_fun/qngd,knd->qngk/dot_general | solution.py:32
  1384.2 14.0 bitcast_add_fusion.1
  1398.3 11.4 bitcast_add_fusion.2
  1434.6 96.6 %collective-permute-done.1 = bf16[1024,8,128]{2,0,1:T(8,128)(2,1)} collective-permute-done((bf16[1024,8,128]{2,0,1:T(8,128)(2,1)}, bf16[1024,8,128]{2,0,1:T(8,128)(2,1)}, u32[]{:S(2)}, u32[]{:S(2)}) %collective-permute-start.1) | collective-permute-done | bytes 2097184 | tf_op jit(solution)/shard_map/while/body/eval_jaxpr/ppermute | solution.py:95
  1534.2 19.4 collective-permute-done
  1555.0 92.3 %conditional.2 = (f32[1024,8,2,128]{3,0,2,1:T(8,128)}, f32[1024,8,128]{2,0,1:T(8,128)}, f32[1024,8,128]{2,0,1:T(8,128)}) conditional(s32[]{:T(128)} %convert_element_type.156, (f32[1024,8,2,128]{3,0,2,1:T(8,128)}, bf16[1024,8,2,128]{3,0,2,1:T(8,128)(2,1)}, bf16[1024,8,128]{2,0,1:T(8,128)(2,1)S(1)}, f32[1024,8,2]{0,2,1:T(2,128)S(1)}, ...), branch_computations={%region_3.3_spmd, %region_4.4_spmd} | conditional | flops 10812391424 | bytes 233013312 | solution.py:99
  1559.7 17.2 fusion.13
  1576.8 17.3 bitcast_add_fusion
  1594.1 21.6 %fusion.1 = bf16[512,8,2,1024]{0,3,2,1:T(8,128)(2,1)} fusion(f32[8,1024,512,2]{2,1,3,0:T(8,128)} %fusion.13, f32[512,8,2]{0,2,1:T(2,128)S(1)} %slice.79, f32[512,8,2]{0,2,1:T(2,128)S(1)} %slice.77, bf16[1024,8,128]{2,0,1:T(8,128)(2,1)} %get-tuple-element.349, bf16[1024,8,2,128]{3,0,2,1:T(8,128)(2,1)} %get-tuple-element.350), kind=kOutput, calls=%fused_computation.2 | convolution fusion | flops 2189426688 | bytes 54591488 | tf_op jit(solution)/shard_map/while/body/eval_jaxpr/cond/branch_0_fun/qngd,knd->qngk/dot_general | solution.py:32
  1615.7 14.0 bitcast_add_fusion.1
  1629.8 11.4 bitcast_add_fusion.2
  1666.1 96.6 %collective-permute-done.1 = bf16[1024,8,128]{2,0,1:T(8,128)(2,1)} collective-permute-done((bf16[1024,8,128]{2,0,1:T(8,128)(2,1)}, bf16[1024,8,128]{2,0,1:T(8,128)(2,1)}, u32[]{:S(2)}, u32[]{:S(2)}) %collective-permute-start.1) | collective-permute-done | bytes 2097184 | tf_op jit(solution)/shard_map/while/body/eval_jaxpr/ppermute | solution.py:95
  1765.7 19.4 collective-permute-done
  1786.5 92.4 %conditional.2 = (f32[1024,8,2,128]{3,0,2,1:T(8,128)}, f32[1024,8,128]{2,0,1:T(8,128)}, f32[1024,8,128]{2,0,1:T(8,128)}) conditional(s32[]{:T(128)} %convert_element_type.156, (f32[1024,8,2,128]{3,0,2,1:T(8,128)}, bf16[1024,8,2,128]{3,0,2,1:T(8,128)(2,1)}, bf16[1024,8,128]{2,0,1:T(8,128)(2,1)S(1)}, f32[1024,8,2]{0,2,1:T(2,128)S(1)}, ...), branch_computations={%region_3.3_spmd, %region_4.4_spmd} | conditional | flops 10812391424 | bytes 233013312 | solution.py:99
  1791.2 17.2 fusion.13
  1808.3 17.3 bitcast_add_fusion
  1825.6 21.6 %fusion.1 = bf16[512,8,2,1024]{0,3,2,1:T(8,128)(2,1)} fusion(f32[8,1024,512,2]{2,1,3,0:T(8,128)} %fusion.13, f32[512,8,2]{0,2,1:T(2,128)S(1)} %slice.79, f32[512,8,2]{0,2,1:T(2,128)S(1)} %slice.77, bf16[1024,8,128]{2,0,1:T(8,128)(2,1)} %get-tuple-element.349, bf16[1024,8,2,128]{3,0,2,1:T(8,128)(2,1)} %get-tuple-element.350), kind=kOutput, calls=%fused_computation.2 | convolution fusion | flops 2189426688 | bytes 54591488 | tf_op jit(solution)/shard_map/while/body/eval_jaxpr/cond/branch_0_fun/qngd,knd->qngk/dot_general | solution.py:32
  1847.3 14.0 bitcast_add_fusion.1
  1861.3 11.4 bitcast_add_fusion.2
  1904.4 14.4 copy.101
  1926.9 27.7 %fusion.56 = (f32[128]{0:T(128)S(1)}, f32[1024,16]{1,0:T(8,128)}, f32[1024,16,128]{2,1,0:T(8,128)}) fusion(bf16[1024,16,128]{2,1,0:T(8,128)(2,1)S(1)} %copy-done.2, f32[1024,16]{1,0:T(8,128)S(1)} %copy-done.18, f32[128]{0:T(128)S(1)} %copy-done.39, f32[1024,16,64]{2,1,0:T(8,128)} %get-tuple-element.482, f32[1024,16,64]{2,1,0:T(8,128)} %get-tuple-element.481, ...), kind=kLoop, calls=%fused_computation.74 | loop fusion | flops 20955008 | bytes 30016512 | tf_op jit(solution)/shard_map/transpose(jvp())/reduce_sum | solution.py:20
  1982.3 25.2 %all-reduce.4 = (f32[128]{0:T(128)}, f32[128]{0:T(128)}) all-reduce(f32[128]{0:T(128)S(1)} %get-tuple-element.445, f32[128]{0:T(128)S(1)} %get-tuple-element.447), channel_id=1, replica_groups=mesh['dp'=2,'cp'=8] {'cp'}, use_global_device_ids=true, to_apply=%region_9.10 | all-reduce | flops 256 | bytes 2048 | tf_op jit(solution)/shard_map/psum | solution.py:109
  (260 shorter events, 424.7 us)
Async XLA Ops:
  10.2 5.4 copy-start.10
  20.2 8.7 copy-start.40
  20.2 36.0 %copy-start.30 = (f32[1024,8]{0,1:T(8,128)}, f32[1024,8]{0,1:T(8,128)S(1)}, u32[]{:S(2)}) copy-start(f32[1024,8]{0,1:T(8,128)S(1)} %fusion.97) | copy-start | bytes 98308
  25.1 17.0 copy-start.17
  29.0 27.3 %copy-start.19 = (f32[1024,128]{1,0:T(8,128)}, f32[1024,128]{1,0:T(8,128)S(1)}, u32[]{:S(2)}) copy-start(f32[1024,128]{1,0:T(8,128)S(1)} %get-tuple-element.493) | copy-start | bytes 1572868
  30.1 4.7 copy-start.1
  30.1 4.7 copy-start.38
  52.6 4.4 copy-start.14
  52.6 5.7 copy-start.15
  61.8 8.1 copy-start.6
  69.9 8.1 copy-start.37
  123.4 4.2 copy-start.7
  127.6 8.1 copy-start.9
  154.7 13.1 slice-start
  154.7 15.9 slice-start.2
  160.1 7.7 slice-start.1
  160.1 10.5 slice-start.3
  174.0 12.7 copy-start.12
  186.7 7.7 copy-start.13
  201.2 9.3 copy-start.16
  214.7 5.5 copy-start.29
  247.7 139.3 %collective-permute-start.3 = (f32[1024,8,128]{2,0,1:T(8,128)}, f32[1024,8,128]{2,0,1:T(8,128)}, u32[]{:S(2)}, u32[]{:S(2)}) collective-permute-start(f32[1024,8,128]{2,0,1:T(8,128)} %get-tuple-element.614), channel_id=1, source_target_pairs={{0,1},{1,2},{2,3},{3,4},{4,5},{5,6},{6,7},{7,0},{8,9},{9,10},{10,1... | collective-permute-start | bytes 12582920 | tf_op jit(solution)/shard_map/while/body/eval_jaxpr/ppermute | solution.py:97
  250.4 136.6 %collective-permute-start.2 = (f32[1024,8,128]{2,0,1:T(8,128)}, f32[1024,8,128]{2,0,1:T(8,128)}, u32[]{:S(2)}, u32[]{:S(2)}) collective-permute-start(f32[1024,8,128]{2,0,1:T(8,128)} %get-tuple-element.613), channel_id=1, source_target_pairs={{0,1},{1,2},{2,3},{3,4},{4,5},{5,6},{6,7},{7,0},{8,9},{9,10},{10,1... | collective-permute-start | bytes 12582920 | tf_op jit(solution)/shard_map/while/body/eval_jaxpr/ppermute | solution.py:96
  250.5 112.8 %collective-permute-start.1 = (bf16[1024,8,128]{2,0,1:T(8,128)(2,1)}, bf16[1024,8,128]{2,0,1:T(8,128)(2,1)}, u32[]{:S(2)}, u32[]{:S(2)}) collective-permute-start(bf16[1024,8,128]{2,0,1:T(8,128)(2,1)} %get-tuple-element.611), channel_id=1, source_target_pairs={{0,1},{1,2},{2,3},{3,4},{4,5},{5,6},{6,7},{7,0},{8,9},{9,10},{10,1... | collective-permute-start | bytes 6291464 | tf_op jit(solution)/shard_map/while/body/eval_jaxpr/ppermute | solution.py:95
  252.2 133.6 %collective-permute-start = (bf16[1024,8,128]{2,0,1:T(8,128)(2,1)}, bf16[1024,8,128]{2,0,1:T(8,128)(2,1)S(1)}, u32[]{:S(2)}, u32[]{:S(2)}) collective-permute-start(bf16[1024,8,128]{2,0,1:T(8,128)(2,1)} %get-tuple-element.610), channel_id=1, source_target_pairs={{0,1},{1,2},{2,3},{3,4},{4,5},{5,6},{6,7},{7,0},{8,9},{9,10},{10,1... | collective-permute-start | bytes 6291464 | tf_op jit(solution)/shard_map/while/body/eval_jaxpr/ppermute | solution.py:94
  484.6 139.1 %collective-permute-start.3 = (f32[1024,8,128]{2,0,1:T(8,128)}, f32[1024,8,128]{2,0,1:T(8,128)}, u32[]{:S(2)}, u32[]{:S(2)}) collective-permute-start(f32[1024,8,128]{2,0,1:T(8,128)} %get-tuple-element.614), channel_id=1, source_target_pairs={{0,1},{1,2},{2,3},{3,4},{4,5},{5,6},{6,7},{7,0},{8,9},{9,10},{10,1... | collective-permute-start | bytes 12582920 | tf_op jit(solution)/shard_map/while/body/eval_jaxpr/ppermute | solution.py:97
  487.1 136.6 %collective-permute-start.2 = (f32[1024,8,128]{2,0,1:T(8,128)}, f32[1024,8,128]{2,0,1:T(8,128)}, u32[]{:S(2)}, u32[]{:S(2)}) collective-permute-start(f32[1024,8,128]{2,0,1:T(8,128)} %get-tuple-element.613), channel_id=1, source_target_pairs={{0,1},{1,2},{2,3},{3,4},{4,5},{5,6},{6,7},{7,0},{8,9},{9,10},{10,1... | collective-permute-start | bytes 12582920 | tf_op jit(solution)/shard_map/while/body/eval_jaxpr/ppermute | solution.py:96
  487.1 112.8 %collective-permute-start.1 = (bf16[1024,8,128]{2,0,1:T(8,128)(2,1)}, bf16[1024,8,128]{2,0,1:T(8,128)(2,1)}, u32[]{:S(2)}, u32[]{:S(2)}) collective-permute-start(bf16[1024,8,128]{2,0,1:T(8,128)(2,1)} %get-tuple-element.611), channel_id=1, source_target_pairs={{0,1},{1,2},{2,3},{3,4},{4,5},{5,6},{6,7},{7,0},{8,9},{9,10},{10,1... | collective-permute-start | bytes 6291464 | tf_op jit(solution)/shard_map/while/body/eval_jaxpr/ppermute | solution.py:95
  488.9 133.6 %collective-permute-start = (bf16[1024,8,128]{2,0,1:T(8,128)(2,1)}, bf16[1024,8,128]{2,0,1:T(8,128)(2,1)S(1)}, u32[]{:S(2)}, u32[]{:S(2)}) collective-permute-start(bf16[1024,8,128]{2,0,1:T(8,128)(2,1)} %get-tuple-element.610), channel_id=1, source_target_pairs={{0,1},{1,2},{2,3},{3,4},{4,5},{5,6},{6,7},{7,0},{8,9},{9,10},{10,1... | collective-permute-start | bytes 6291464 | tf_op jit(solution)/shard_map/while/body/eval_jaxpr/ppermute | solution.py:94
  698.5 11.4 copy-start
  716.1 144.3 %collective-permute-start.3 = (f32[1024,8,128]{2,0,1:T(8,128)}, f32[1024,8,128]{2,0,1:T(8,128)}, u32[]{:S(2)}, u32[]{:S(2)}) collective-permute-start(f32[1024,8,128]{2,0,1:T(8,128)} %get-tuple-element.614), channel_id=1, source_target_pairs={{0,1},{1,2},{2,3},{3,4},{4,5},{5,6},{6,7},{7,0},{8,9},{9,10},{10,1... | collective-permute-start | bytes 12582920 | tf_op jit(solution)/shard_map/while/body/eval_jaxpr/ppermute | solution.py:97
  723.8 136.6 %collective-permute-start.2 = (f32[1024,8,128]{2,0,1:T(8,128)}, f32[1024,8,128]{2,0,1:T(8,128)}, u32[]{:S(2)}, u32[]{:S(2)}) collective-permute-start(f32[1024,8,128]{2,0,1:T(8,128)} %get-tuple-element.613), channel_id=1, source_target_pairs={{0,1},{1,2},{2,3},{3,4},{4,5},{5,6},{6,7},{7,0},{8,9},{9,10},{10,1... | collective-permute-start | bytes 12582920 | tf_op jit(solution)/shard_map/while/body/eval_jaxpr/ppermute | solution.py:96
  723.8 112.8 %collective-permute-start.1 = (bf16[1024,8,128]{2,0,1:T(8,128)(2,1)}, bf16[1024,8,128]{2,0,1:T(8,128)(2,1)}, u32[]{:S(2)}, u32[]{:S(2)}) collective-permute-start(bf16[1024,8,128]{2,0,1:T(8,128)(2,1)} %get-tuple-element.611), channel_id=1, source_target_pairs={{0,1},{1,2},{2,3},{3,4},{4,5},{5,6},{6,7},{7,0},{8,9},{9,10},{10,1... | collective-permute-start | bytes 6291464 | tf_op jit(solution)/shard_map/while/body/eval_jaxpr/ppermute | solution.py:95
  725.6 133.6 %collective-permute-start = (bf16[1024,8,128]{2,0,1:T(8,128)(2,1)}, bf16[1024,8,128]{2,0,1:T(8,128)(2,1)S(1)}, u32[]{:S(2)}, u32[]{:S(2)}) collective-permute-start(bf16[1024,8,128]{2,0,1:T(8,128)(2,1)} %get-tuple-element.610), channel_id=1, source_target_pairs={{0,1},{1,2},{2,3},{3,4},{4,5},{5,6},{6,7},{7,0},{8,9},{9,10},{10,1... | collective-permute-start | bytes 6291464 | tf_op jit(solution)/shard_map/while/body/eval_jaxpr/ppermute | solution.py:94
  935.2 11.4 copy-start
  952.8 139.2 %collective-permute-start.3 = (f32[1024,8,128]{2,0,1:T(8,128)}, f32[1024,8,128]{2,0,1:T(8,128)}, u32[]{:S(2)}, u32[]{:S(2)}) collective-permute-start(f32[1024,8,128]{2,0,1:T(8,128)} %get-tuple-element.614), channel_id=1, source_target_pairs={{0,1},{1,2},{2,3},{3,4},{4,5},{5,6},{6,7},{7,0},{8,9},{9,10},{10,1... | collective-permute-start | bytes 12582920 | tf_op jit(solution)/shard_map/while/body/eval_jaxpr/ppermute | solution.py:97
  955.3 136.6 %collective-permute-start.2 = (f32[1024,8,128]{2,0,1:T(8,128)}, f32[1024,8,128]{2,0,1:T(8,128)}, u32[]{:S(2)}, u32[]{:S(2)}) collective-permute-start(f32[1024,8,128]{2,0,1:T(8,128)} %get-tuple-element.613), channel_id=1, source_target_pairs={{0,1},{1,2},{2,3},{3,4},{4,5},{5,6},{6,7},{7,0},{8,9},{9,10},{10,1... | collective-permute-start | bytes 12582920 | tf_op jit(solution)/shard_map/while/body/eval_jaxpr/ppermute | solution.py:96
  959.7 108.4 %collective-permute-start.1 = (bf16[1024,8,128]{2,0,1:T(8,128)(2,1)}, bf16[1024,8,128]{2,0,1:T(8,128)(2,1)}, u32[]{:S(2)}, u32[]{:S(2)}) collective-permute-start(bf16[1024,8,128]{2,0,1:T(8,128)(2,1)} %get-tuple-element.611), channel_id=1, source_target_pairs={{0,1},{1,2},{2,3},{3,4},{4,5},{5,6},{6,7},{7,0},{8,9},{9,10},{10,1... | collective-permute-start | bytes 6291464 | tf_op jit(solution)/shard_map/while/body/eval_jaxpr/ppermute | solution.py:95
  962.3 128.4 %collective-permute-start = (bf16[1024,8,128]{2,0,1:T(8,128)(2,1)}, bf16[1024,8,128]{2,0,1:T(8,128)(2,1)S(1)}, u32[]{:S(2)}, u32[]{:S(2)}) collective-permute-start(bf16[1024,8,128]{2,0,1:T(8,128)(2,1)} %get-tuple-element.610), channel_id=1, source_target_pairs={{0,1},{1,2},{2,3},{3,4},{4,5},{5,6},{6,7},{7,0},{8,9},{9,10},{10,1... | collective-permute-start | bytes 6291464 | tf_op jit(solution)/shard_map/while/body/eval_jaxpr/ppermute | solution.py:94
  1166.8 11.4 copy-start
  1184.3 139.1 %collective-permute-start.3 = (f32[1024,8,128]{2,0,1:T(8,128)}, f32[1024,8,128]{2,0,1:T(8,128)}, u32[]{:S(2)}, u32[]{:S(2)}) collective-permute-start(f32[1024,8,128]{2,0,1:T(8,128)} %get-tuple-element.614), channel_id=1, source_target_pairs={{0,1},{1,2},{2,3},{3,4},{4,5},{5,6},{6,7},{7,0},{8,9},{9,10},{10,1... | collective-permute-start | bytes 12582920 | tf_op jit(solution)/shard_map/while/body/eval_jaxpr/ppermute | solution.py:97
  1186.8 136.6 %collective-permute-start.2 = (f32[1024,8,128]{2,0,1:T(8,128)}, f32[1024,8,128]{2,0,1:T(8,128)}, u32[]{:S(2)}, u32[]{:S(2)}) collective-permute-start(f32[1024,8,128]{2,0,1:T(8,128)} %get-tuple-element.613), channel_id=1, source_target_pairs={{0,1},{1,2},{2,3},{3,4},{4,5},{5,6},{6,7},{7,0},{8,9},{9,10},{10,1... | collective-permute-start | bytes 12582920 | tf_op jit(solution)/shard_map/while/body/eval_jaxpr/ppermute | solution.py:96
  1191.2 108.4 %collective-permute-start.1 = (bf16[1024,8,128]{2,0,1:T(8,128)(2,1)}, bf16[1024,8,128]{2,0,1:T(8,128)(2,1)}, u32[]{:S(2)}, u32[]{:S(2)}) collective-permute-start(bf16[1024,8,128]{2,0,1:T(8,128)(2,1)} %get-tuple-element.611), channel_id=1, source_target_pairs={{0,1},{1,2},{2,3},{3,4},{4,5},{5,6},{6,7},{7,0},{8,9},{9,10},{10,1... | collective-permute-start | bytes 6291464 | tf_op jit(solution)/shard_map/while/body/eval_jaxpr/ppermute | solution.py:95
  1199.0 123.2 %collective-permute-start = (bf16[1024,8,128]{2,0,1:T(8,128)(2,1)}, bf16[1024,8,128]{2,0,1:T(8,128)(2,1)S(1)}, u32[]{:S(2)}, u32[]{:S(2)}) collective-permute-start(bf16[1024,8,128]{2,0,1:T(8,128)(2,1)} %get-tuple-element.610), channel_id=1, source_target_pairs={{0,1},{1,2},{2,3},{3,4},{4,5},{5,6},{6,7},{7,0},{8,9},{9,10},{10,1... | collective-permute-start | bytes 6291464 | tf_op jit(solution)/shard_map/while/body/eval_jaxpr/ppermute | solution.py:94
  1398.3 11.4 copy-start
  1415.8 139.1 %collective-permute-start.3 = (f32[1024,8,128]{2,0,1:T(8,128)}, f32[1024,8,128]{2,0,1:T(8,128)}, u32[]{:S(2)}, u32[]{:S(2)}) collective-permute-start(f32[1024,8,128]{2,0,1:T(8,128)} %get-tuple-element.614), channel_id=1, source_target_pairs={{0,1},{1,2},{2,3},{3,4},{4,5},{5,6},{6,7},{7,0},{8,9},{9,10},{10,1... | collective-permute-start | bytes 12582920 | tf_op jit(solution)/shard_map/while/body/eval_jaxpr/ppermute | solution.py:97
  1418.3 136.6 %collective-permute-start.2 = (f32[1024,8,128]{2,0,1:T(8,128)}, f32[1024,8,128]{2,0,1:T(8,128)}, u32[]{:S(2)}, u32[]{:S(2)}) collective-permute-start(f32[1024,8,128]{2,0,1:T(8,128)} %get-tuple-element.613), channel_id=1, source_target_pairs={{0,1},{1,2},{2,3},{3,4},{4,5},{5,6},{6,7},{7,0},{8,9},{9,10},{10,1... | collective-permute-start | bytes 12582920 | tf_op jit(solution)/shard_map/while/body/eval_jaxpr/ppermute | solution.py:96
  1427.9 103.2 %collective-permute-start.1 = (bf16[1024,8,128]{2,0,1:T(8,128)(2,1)}, bf16[1024,8,128]{2,0,1:T(8,128)(2,1)}, u32[]{:S(2)}, u32[]{:S(2)}) collective-permute-start(bf16[1024,8,128]{2,0,1:T(8,128)(2,1)} %get-tuple-element.611), channel_id=1, source_target_pairs={{0,1},{1,2},{2,3},{3,4},{4,5},{5,6},{6,7},{7,0},{8,9},{9,10},{10,1... | collective-permute-start | bytes 6291464 | tf_op jit(solution)/shard_map/while/body/eval_jaxpr/ppermute | solution.py:95
  1430.5 123.2 %collective-permute-start = (bf16[1024,8,128]{2,0,1:T(8,128)(2,1)}, bf16[1024,8,128]{2,0,1:T(8,128)(2,1)S(1)}, u32[]{:S(2)}, u32[]{:S(2)}) collective-permute-start(bf16[1024,8,128]{2,0,1:T(8,128)(2,1)} %get-tuple-element.610), channel_id=1, source_target_pairs={{0,1},{1,2},{2,3},{3,4},{4,5},{5,6},{6,7},{7,0},{8,9},{9,10},{10,1... | collective-permute-start | bytes 6291464 | tf_op jit(solution)/shard_map/while/body/eval_jaxpr/ppermute | solution.py:94
  1629.8 11.4 copy-start
  1647.3 139.1 %collective-permute-start.3 = (f32[1024,8,128]{2,0,1:T(8,128)}, f32[1024,8,128]{2,0,1:T(8,128)}, u32[]{:S(2)}, u32[]{:S(2)}) collective-permute-start(f32[1024,8,128]{2,0,1:T(8,128)} %get-tuple-element.614), channel_id=1, source_target_pairs={{0,1},{1,2},{2,3},{3,4},{4,5},{5,6},{6,7},{7,0},{8,9},{9,10},{10,1... | collective-permute-start | bytes 12582920 | tf_op jit(solution)/shard_map/while/body/eval_jaxpr/ppermute | solution.py:97
  1649.8 136.6 %collective-permute-start.2 = (f32[1024,8,128]{2,0,1:T(8,128)}, f32[1024,8,128]{2,0,1:T(8,128)}, u32[]{:S(2)}, u32[]{:S(2)}) collective-permute-start(f32[1024,8,128]{2,0,1:T(8,128)} %get-tuple-element.613), channel_id=1, source_target_pairs={{0,1},{1,2},{2,3},{3,4},{4,5},{5,6},{6,7},{7,0},{8,9},{9,10},{10,1... | collective-permute-start | bytes 12582920 | tf_op jit(solution)/shard_map/while/body/eval_jaxpr/ppermute | solution.py:96
  1659.5 103.2 %collective-permute-start.1 = (bf16[1024,8,128]{2,0,1:T(8,128)(2,1)}, bf16[1024,8,128]{2,0,1:T(8,128)(2,1)}, u32[]{:S(2)}, u32[]{:S(2)}) collective-permute-start(bf16[1024,8,128]{2,0,1:T(8,128)(2,1)} %get-tuple-element.611), channel_id=1, source_target_pairs={{0,1},{1,2},{2,3},{3,4},{4,5},{5,6},{6,7},{7,0},{8,9},{9,10},{10,1... | collective-permute-start | bytes 6291464 | tf_op jit(solution)/shard_map/while/body/eval_jaxpr/ppermute | solution.py:95
  1662.0 123.2 %collective-permute-start = (bf16[1024,8,128]{2,0,1:T(8,128)(2,1)}, bf16[1024,8,128]{2,0,1:T(8,128)(2,1)S(1)}, u32[]{:S(2)}, u32[]{:S(2)}) collective-permute-start(bf16[1024,8,128]{2,0,1:T(8,128)(2,1)} %get-tuple-element.610), channel_id=1, source_target_pairs={{0,1},{1,2},{2,3},{3,4},{4,5},{5,6},{6,7},{7,0},{8,9},{9,10},{10,1... | collective-permute-start | bytes 6291464 | tf_op jit(solution)/shard_map/while/body/eval_jaxpr/ppermute | solution.py:94
  1861.3 11.4 copy-start
  1886.3 79.9 %collective-permute-start.4 = (f32[1024,8,128]{2,0,1:T(8,128)}, f32[1024,8,128]{2,0,1:T(8,128)}, u32[]{:S(2)}, u32[]{:S(2)}) collective-permute-start(f32[1024,8,128]{2,0,1:T(8,128)} %get-tuple-element.389), channel_id=1, source_target_pairs={{0,1},{1,2},{2,3},{3,4},{4,5},{5,6},{6,7},{7,0},{8,9},{9,10},{10,1... | collective-permute-start | bytes 12582920 | tf_op jit(solution)/shard_map/ppermute | solution.py:104
  1894.8 71.4 %collective-permute-start.5 = (bf16[1024,8,128]{2,1,0:T(8,128)(2,1)}, bf16[1024,8,128]{2,1,0:T(8,128)(2,1)}, u32[]{:S(2)}, u32[]{:S(2)}) collective-permute-start(bf16[1024,8,128]{2,1,0:T(8,128)(2,1)} %copy.104), channel_id=1, source_target_pairs={{0,1},{1,2},{2,3},{3,4},{4,5},{5,6},{6,7},{7,0},{8,9},{9,10},{10,1... | collective-permute-start | bytes 6291464 | tf_op jit(solution)/shard_map/ppermute | solution.py:105
  1904.4 14.5 copy-start.22
  1919.7 7.1 copy-start.2
  1919.7 7.1 copy-start.18
  1919.8 7.1 copy-start.20
  1919.8 7.1 copy-start.39
  1956.9 9.3 copy-start.23
  1970.4 5.4 copy-start.36
  (17 other events, 45.7 us)
where the time goes:
time: 2020 us; the launch traced here: 2010 us
  waiting for transfers between devices  869 us (43%)
  matrix products  692 us (34%)
  other arithmetic  159 us (8%)
  local copies, waits for them, and re-layouts  141 us (7%)
  starting transfers between devices  92.1 us (5%)
  loops' own time  31.2 us (2%)
  blocking collectives  25.2 us (1%)
    ppermute x7, waiting for transfers between devices, visit_source(): v_cur = lax.ppermute(v_cur, 'cp', shift_pairs)  733 us
    dot_general x10, matrix products, pair_grads(): jnp.einsum('qngd,knd->qngk', do_blk, v_blk, preferred_element_type=jnp.fl...  182 us
    dot_general x10, matrix products, pair_grads(): jnp.einsum('qngk,qngd->knd', prob_bf, do_blk, preferred_element_type=jnp....  154 us
    dot_general x10, matrix products, pair_grads(): jnp.einsum('qngd,knd->qngk', q_blk, k_blk, preferred_element_type=jnp.flo...  145 us
    ppermute x7, waiting for transfers between devices, visit_source(): k_cur = lax.ppermute(k_cur, 'cp', shift_pairs)  136 us
    dot_general x10, matrix products, pair_grads(): jnp.einsum('qngk,qngd->knd', score_grad, q_blk, preferred_element_type=jn...  119 us
    dot_general x10, matrix products, pair_grads(): jnp.einsum('qngk,knd->qngd', score_grad, k_blk, preferred_element_type=jn...  91.4 us
    while x6, local copies, waits for them, and re-layouts, local_grads(): lax.fori_loop(1, cp_size, visit_source, (k_b, v_proj, dq_acc, dk_acc, dv_...  43.9 us
  transfers between devices with their start and end apart: 30, of which 14 were waited for; matrix products, arithmetic and copies ran while one was open for 5% of the time, Pallas kernels for 0%

commit v1 on v0

v1 whole, which is shorter than its diff:
```python
import functools

import jax
import jax.numpy as jnp
from jax import lax
from jax.experimental import pallas as pl
from jax.experimental.pallas import tpu as pltpu
from jax.sharding import PartitionSpec as P

HEAD_DIM = 128
ROPE_THETA = 1000000.0
NORM_EPS = 1e-6
SM_SCALE = HEAD_DIM ** -0.5
F32 = jnp.float32
BF16 = jnp.bfloat16


def angle_tables(positions):
    inv_freq = ROPE_THETA ** (-jnp.arange(0, HEAD_DIM, 2).astype(F32) / HEAD_DIM)
    angles = positions.astype(F32)[:, None] * inv_freq[None, :]
    angles = jnp.concatenate([angles, angles], axis=-1)
    return jnp.cos(angles), jnp.sin(angles)


def lane_sign():
    lane = lax.broadcasted_iota(jnp.int32, (1, HEAD_DIM), 1)
    return jnp.where(lane < HEAD_DIM // 2, -1.0, 1.0).astype(F32)


def chunk_angles(c, cos_o, sin_o, cos_c, sin_c):
    cc, sc = cos_c[pl.ds(c, 1), :], sin_c[pl.ds(c, 1), :]
    co, so = cos_o[...], sin_o[...]
    return cc * co - sc * so, (sc * co + cc * so) * lane_sign()


def norm_rope(x, weight, cos_t, sin_s):
    rinv = lax.rsqrt(jnp.mean(x * x, axis=-1, keepdims=True) + NORM_EPS)
    y = x * rinv * weight
    return y * cos_t + pltpu.roll(y, HEAD_DIM // 2, 1) * sin_s


def norm_rope_grad(x, weight, cos_t, sin_s, g):
    rinv = lax.rsqrt(jnp.mean(x * x, axis=-1, keepdims=True) + NORM_EPS)
    n = x * rinv
    dy = g * cos_t + pltpu.roll(g * sin_s, HEAD_DIM // 2, 1)
    dw = dy * n
    dn = dy * weight
    dx = rinv * (dn - n * jnp.mean(dn * n, axis=-1, keepdims=True))
    return dx, jnp.sum(dw.reshape(-1, 8, HEAD_DIM), axis=0)


def split3(x):
    hi = x.astype(BF16).astype(F32)
    mid = (x - hi).astype(BF16).astype(F32)
    return hi, mid, x - hi - mid


def prep_chunk(c, raw, ld, qw, kw, tabs, qr, qt, dot_, ext):
    cos_t, sin_s = chunk_angles(c, *tabs)
    rows = raw.shape[1]
    for h in range(2):
        y = norm_rope(raw[c, :, h * 128:(h + 1) * 128].astype(F32), qw[...], cos_t, sin_s)
        qr[c, :, h * 128:(h + 1) * 128] = y.astype(BF16)
        qt[c, :, h * rows:(h + 1) * rows] = y.T.astype(BF16)
        dot_[c, :, h * rows:(h + 1) * rows] = raw[c, :, 512 + h * 128:640 + h * 128].astype(F32).T.astype(BF16)
    y = norm_rope(raw[c, :, 256:384].astype(F32), kw[...], cos_t, sin_s)
    qr[c, :, 256:384] = y.astype(BF16)
    vals = ld[c]
    parts = []
    for t in range(4):
        parts.extend(split3(vals[t:t + 1] * (1.0 / SM_SCALE if t < 2 else 1.0)))
    parts.append(jnp.zeros((HEAD_DIM - 12, rows), F32))
    ext[c] = jnp.concatenate(parts, axis=0).T.astype(BF16)


def minus_one_lanes(rows, first):
    lane = lax.broadcasted_iota(jnp.int32, (rows, HEAD_DIM), 1)
    return jnp.where((lane >= first) & (lane < first + 3), -1.0, 0.0).astype(BF16)


def dot_t(a, b):
    return lax.dot_general(a, b, (((1,), (1,)), ((), ())), preferred_element_type=F32)


def dot_n(a, b):
    return lax.dot_general(a, b, (((1,), (0,)), ((), ())), preferred_element_type=F32)


def block_grads(i, j, masked, raw, qr, qt, dot_, ext, dq, dkt, dvt):
    rows = raw.shape[1]
    kb = qr[j, :, 256:384]
    vb = raw[j, :, 384:512]
    ex = ext[i]
    probs, grads = [], []
    for h in range(2):
        ke = jnp.concatenate([kb, minus_one_lanes(rows, 3 * h)], axis=1)
        ve = jnp.concatenate([vb, minus_one_lanes(rows, 6 + 3 * h)], axis=1)
        qe = jnp.concatenate([qr[i, :, h * 128:(h + 1) * 128], ex], axis=1)
        de = jnp.concatenate([raw[i, :, 512 + h * 128:640 + h * 128], ex], axis=1)
        s = dot_t(qe, ke)
        if masked:
            r_id = lax.broadcasted_iota(jnp.int32, s.shape, 0)
            c_id = lax.broadcasted_iota(jnp.int32, s.shape, 1)
            s = jnp.where(r_id >= c_id, s, -jnp.inf)
        p = jnp.exp(s * SM_SCALE)
        ds = (p * dot_t(de, ve)).astype(BF16)
        probs.append(p.astype(BF16))
        grads.append(ds)
        dq[i, :, h * 128:(h + 1) * 128] += dot_n(ds, kb)
    dvt[j] += dot_n(dot_[i], jnp.concatenate(probs, axis=0))
    dkt[j] += dot_n(qt[i], jnp.concatenate(grads, axis=0))


def finish_q(c, raw, qw, tabs, dq, dw):
    cos_t, sin_s = chunk_angles(c, *tabs)
    for h in range(2):
        cols = slice(h * 128, (h + 1) * 128)
        dx, part = norm_rope_grad(raw[c, :, cols].astype(F32), qw[...], cos_t, sin_s, dq[c, :, cols] * SM_SCALE)
        raw[c, :, cols] = dx.astype(BF16)
        dw[0:8, :] += part


def finish_k(c, raw, kw, tabs, dkt, dvt, dw):
    cos_t, sin_s = chunk_angles(c, *tabs)
    dx, part = norm_rope_grad(raw[c, :, 256:384].astype(F32), kw[...], cos_t, sin_s, dkt[c].T * SM_SCALE)
    raw[c, :, 256:384] = dx.astype(BF16)
    dw[8:16, :] += part
    raw[c, :, 384:512] = dvt[c].T.astype(BF16)


def attn_kernel(slab, ld_in, qw, kw, cos_o, sin_o, cos_c, sin_c, out, dw,
                raw, ld, qr, qt, dot_, ext, dq, dkt, dvt, sems):
    n_chunks = raw.shape[0]
    half = n_chunks // 2
    tabs = (cos_o, sin_o, cos_c, sin_c)

    def slot(c):
        dev = jnp.minimum(c, n_chunks - 1 - c)
        return dev, (c >= half).astype(jnp.int32)

    def load(c, start):
        dev, part = slot(c)
        one = pltpu.make_async_copy(slab.at[dev, part], raw.at[c], sems.at[c, 0])
        two = pltpu.make_async_copy(ld_in.at[dev, part], ld.at[c], sems.at[c, 1])
        if start:
            one.start()
            two.start()
        else:
            one.wait()
            two.wait()

    lax.fori_loop(0, n_chunks, lambda c, _: (load(c, True), 0)[1], 0)
    dw[...] = jnp.zeros_like(dw)
    dq[...] = jnp.zeros_like(dq)
    dkt[...] = jnp.zeros_like(dkt)
    dvt[...] = jnp.zeros_like(dvt)

    def prep(c, _):
        load(c, False)
        prep_chunk(c, raw, ld, qw, kw, tabs, qr, qt, dot_, ext)
        return 0

    lax.fori_loop(0, n_chunks, prep, 0)

    def column(j, _):
        block_grads(j, j, True, raw, qr, qt, dot_, ext, dq, dkt, dvt)

        def row(i, _):
            block_grads(i, j, False, raw, qr, qt, dot_, ext, dq, dkt, dvt)
            return 0

        lax.fori_loop(j + 1, n_chunks, row, 0)
        return 0

    lax.fori_loop(0, n_chunks, column, 0)

    def finish(c, _):
        finish_q(c, raw, qw, tabs, dq, dw)
        finish_k(c, raw, kw, tabs, dkt, dvt, dw)
        dev, part = slot(c)
        pltpu.make_async_copy(raw.at[c, :, 0:512], out.at[dev, part], sems.at[c, 0]).start()
        return 0

    lax.fori_loop(0, n_chunks, finish, 0)

    def drain(c, _):
        dev, part = slot(c)
        pltpu.make_async_copy(raw.at[c, :, 0:512], out.at[dev, part], sems.at[c, 0]).wait()
        return 0

    lax.fori_loop(0, n_chunks, drain, 0)


def run_attention(slab, ld, q_norm, k_norm, tabs):
    n_dev, _, rows, _ = slab.shape
    n_chunks = 2 * n_dev
    any_spec = pl.BlockSpec(memory_space=pl.ANY)
    vmem_spec = pl.BlockSpec(memory_space=pltpu.VMEM)
    return pl.pallas_call(
        attn_kernel,
        out_shape=(jax.ShapeDtypeStruct((n_dev, 2, rows, 512), BF16), jax.ShapeDtypeStruct((16, HEAD_DIM), F32)),
        in_specs=[any_spec, any_spec] + [vmem_spec] * 6,
        out_specs=(any_spec, vmem_spec),
        scratch_shapes=[
            pltpu.VMEM((n_chunks, rows, 768), BF16),
            pltpu.VMEM((n_chunks, 8, rows), F32),
            pltpu.VMEM((n_chunks, rows, 384), BF16),
            pltpu.VMEM((n_chunks, HEAD_DIM, 2 * rows), BF16),
            pltpu.VMEM((n_chunks, HEAD_DIM, 2 * rows), BF16),
            pltpu.VMEM((n_chunks, rows, HEAD_DIM), BF16),
            pltpu.VMEM((n_chunks, rows, 256), F32),
            pltpu.VMEM((n_chunks, HEAD_DIM, rows), F32),
            pltpu.VMEM((n_chunks, HEAD_DIM, rows), F32),
            pltpu.SemaphoreType.DMA((n_chunks, 2)),
        ],
        compiler_params=pltpu.CompilerParams(vmem_limit_bytes=67043328),
        name='attention_backward',
    )(slab, ld, q_norm, k_norm, *tabs)


def solution(mesh):
    cp_size = mesh.shape['cp']

    def local_grads(q_raw, k_raw, v_proj, out_fwd, lse_fwd, d_out, q_norm, k_norm):
        local_rows, num_heads = q_raw.shape[0], q_raw.shape[1]
        rows = local_rows // 2
        kv_heads = k_raw.shape[1]
        by_group = lambda a: a.reshape(local_rows, kv_heads, -1)
        slab = jnp.concatenate([by_group(q_raw), by_group(k_raw), by_group(v_proj), by_group(d_out)], axis=-1)
        slab = slab.transpose(1, 0, 2)
        delta = jnp.einsum('thd,thd->th', d_out, out_fwd, preferred_element_type=F32)
        ld = jnp.concatenate([lse_fwd.reshape(local_rows, kv_heads, 2), delta.reshape(local_rows, kv_heads, 2)], axis=-1)
        ld = jnp.pad(ld, ((0, 0), (0, 0), (0, 4))).reshape(2, rows, kv_heads, 8).transpose(2, 0, 3, 1)
        slab = lax.all_to_all(slab, 'cp', 0, 0)
        ld = lax.all_to_all(ld, 'cp', 0, 0)
        slab = slab.reshape(cp_size, 2, rows, 768)
        tabs = angle_tables(jnp.arange(rows)) + angle_tables(jnp.arange(2 * cp_size) * rows)
        out, dw = run_attention(slab, ld, q_norm.reshape(1, -1), k_norm.reshape(1, -1), tabs)
        out = lax.all_to_all(out, 'cp', 0, 0)
        out = out.reshape(kv_heads, local_rows, 512)
        dq_raw = out[..., :256].transpose(1, 0, 2).reshape(local_rows, num_heads, HEAD_DIM)
        dk_raw = out[..., 256:384].transpose(1, 0, 2)
        dv = out[..., 384:].transpose(1, 0, 2)
        dw = lax.psum(jnp.stack([dw[:8].sum(0), dw[8:].sum(0)]), 'cp')
        return dq_raw, dk_raw, dv, dw[0], dw[1]

    row_spec = P(('dp', 'cp'))
    in_specs = (row_spec, row_spec, row_spec, row_spec, row_spec, row_spec, P(), P())
    out_specs = (row_spec, row_spec, row_spec, P('dp'), P('dp'))
    return jax.shard_map(local_grads, mesh=mesh, in_specs=in_specs, out_specs=out_specs, check_vma=False)
```

time: 2020 us -> 533 us (0.26)
  waiting for transfers between devices: 869 us -> 136 us
  matrix products: 692 us -> 0 us
  Pallas kernels: 0 us -> 212 us
  other arithmetic: 159 us -> 14.6 us
  local copies, waits for them, and re-layouts: 141 us -> 52.3 us
  starting transfers between devices: 92.1 us -> 17.4 us
  blocking collectives: 25.2 us -> 98 us
  loops' own time: 31.2 us -> 0 us
    ppermute x30 -> x0, waiting for transfers between devices: 869 us -> none  [the longest x7 733 us: visit_source(): v_cur = lax.ppermute(v_cur, 'cp', shift_pairs)]
    dot_general x50 -> x0, matrix products: 692 us -> none  [the longest x10 182 us: pair_grads(): jnp.einsum('qngd,knd->qngk', do_blk, v_blk, preferred_element_type=jnp.fl...]
    pallas_call x0 -> x1, Pallas kernels: none -> 212 us  [run_attention(): pl.pallas_call(attn_kernel, out_shape=(jax.ShapeDtypeStruct((n_dev, 2, ro...]
    all_to_all x0 -> x3, waiting for transfers between devices: none -> 136 us  [the longest x1 136 us: local_grads(): slab = lax.all_to_all(slab, 'cp', 0, 0)]
    ppermute x30 -> x0, starting transfers between devices: 92.1 us -> none  [the longest x7 28.2 us: visit_source(): dk_cur = lax.ppermute(dk_cur, 'cp', shift_pairs)]
    while x20 -> x0, local copies, waits for them, and re-layouts: 74.6 us -> none  [the longest x6 43.9 us: local_grads(): lax.fori_loop(1, cp_size, visit_source, (k_b, v_proj, dq_acc, dk_acc, dv_...]
    psum x1, blocking collectives: 25.2 us -> 98 us  [local_grads(): dw = lax.psum(jnp.stack([dw[:8].sum(0), dw[8:].sum(0)]), 'cp')]
    concatenate x10 -> x1, other arithmetic: 59.3 us -> 0.77 us  [local_grads(): jnp.concatenate([lse_fwd.reshape(local_rows, kv_heads, 2), delta.reshape(...]
  transfers between devices with their start and end apart: 30 -> 3, of which waited for: 14 -> 1; matrix products, arithmetic and copies ran while one was open for 5% -> 6% of each run, Pallas kernels for 0% -> 0%
where the time goes in v1:
time: 533 us; the launch traced here: 531 us
  Pallas kernels  212 us (40%)
  waiting for transfers between devices  136 us (26%)
  blocking collectives  98 us (18%)
  local copies, waits for them, and re-layouts  52.3 us (10%)
  starting transfers between devices  17.4 us (3%)
  other arithmetic  14.6 us (3%)
    pallas_call x1, Pallas kernels, run_attention(): pl.pallas_call(attn_kernel, out_shape=(jax.ShapeDtypeStruct((n_dev, 2, ro...  212 us
    all_to_all x1, waiting for transfers between devices, local_grads(): slab = lax.all_to_all(slab, 'cp', 0, 0)  136 us
    psum x1, blocking collectives, local_grads(): dw = lax.psum(jnp.stack([dw[:8].sum(0), dw[8:].sum(0)]), 'cp')  98 us
    reshape x4, local copies, waits for them, and re-layouts, local_grads(): by_group = lambda a: a.reshape(local_rows, kv_heads, -1)  22.5 us
  transfers between devices with their start and end apart: 3, of which 1 were waited for; matrix products, arithmetic and copies ran while one was open for 6% of the time, Pallas kernels for 0%

profile of v1, /device:TPU:113, one launch (start us, length us, event | category | flops | bytes accessed | tf_op | source)
XLA Modules:
  0.0 530.9 jit_solution(14436603838123791711)
XLA Ops:
  0.6 0.0 copy-start.5
  0.6 5.7 %fusion = f32[1024,16]{1,0:T(8,128)S(1)} fusion(bf16[1024,16,128]{2,1,0:T(8,128)(2,1)} %param.13, bf16[1024,16,128]{2,1,0:T(8,128)(2,1)} %param.11), kind=kLoop, calls=%fused_computation.2 | loop fusion | flops 8372224 | bytes 8454144
  6.4 0.2 copy.24
  6.6 0.0 copy-done.5
  6.7 0.8 select_maximum_fusion
  7.4 6.0 %all-to-all-start.1 = ((f32[8,2,8,512]{3,2,1,0:T(8,128)}), f32[8,2,8,512]{3,2,1,0:T(8,128)S(1)}, u32[]{:S(2)}, u32[]{:S(2)}) async-start(f32[8,2,8,512]{3,2,1,0:T(8,128)} %bitcast.3), calls=%async_computation.1 | async-start | bytes 524288 | tf_op jit(solution)/shard_map/all_to_all | solution.py:235
  13.4 7.1 %reshape.58 = bf16[1024,8,256]{2,1,0:T(8,128)(2,1)} reshape(bf16[1024,16,128]{2,1,0:T(8,128)(2,1)} %param.13) | data formatting | bytes 8388608 | tf_op jit(solution)/shard_map/reshape | solution.py:228
  20.5 0.0 copy-start.2
  20.5 5.1 copy.16
  25.7 0.0 copy-done.2
  25.7 0.0 copy-start.3
  25.7 0.3 copy.15
  25.9 1.3 copy-done.3
  27.2 1.7 copy.14
  28.9 7.1 %reshape.57 = bf16[1024,8,256]{2,1,0:T(8,128)(2,1)} reshape(bf16[1024,16,128]{2,1,0:T(8,128)(2,1)} %param.8) | data formatting | bytes 8388608 | tf_op jit(solution)/shard_map/reshape | solution.py:228
  36.0 0.0 copy-start
  36.0 0.0 copy-start.1
  36.0 3.2 copy.13
  39.2 0.2 copy-done
  39.4 0.7 copy-done.1
  40.1 5.3 maximum_bitcast_fusion
  45.4 0.0 all-to-all-done.1.ld_in
  45.4 0.0 copy-start.4
  45.4 0.7 copy-done.4
  46.1 5.6 %all-to-all-start = ((bf16[8,1024,768]{2,1,0:T(8,128)(2,1)}), bf16[8,1024,768]{2,1,0:T(8,128)(2,1)}, u32[]{:S(2)}, u32[]{:S(2)}) async-start(bf16[8,1024,768]{2,1,0:T(8,128)(2,1)} %maximum_bitcast_fusion), calls=%async_computation | async-start | bytes 25165824 | tf_op jit(solution)/shard_map/all_to_all | solution.py:234
  51.7 0.1 broadcast_multiply_fusion.1
  51.8 0.7 fusion.3
  52.5 0.1 broadcast_multiply_fusion
  52.7 1.8 fusion.1
  54.5 135.7 %all-to-all-done = bf16[8,1024,768]{2,1,0:T(8,128)(2,1)} async-done(((bf16[8,1024,768]{2,1,0:T(8,128)(2,1)}), bf16[8,1024,768]{2,1,0:T(8,128)(2,1)}, u32[]{:S(2)}, u32[]{:S(2)}) %all-to-all-start) | async-done | bytes 12582944 | tf_op jit(solution)/shard_map/all_to_all | solution.py:234
  190.2 212.1 %attention_backward.1 = (bf16[8,2,512,512]{3,2,1,0:T(8,128)(2,1)}, f32[16,128]{1,0:T(8,128)}) custom-call(bf16[8,2,512,768]{3,2,1,0:T(8,128)(2,1)} %bitcast.1.slab, f32[8,2,8,512]{3,2,1,0:T(8,128)} %copy-done.4, f32[1,128]{1,0:T(1,128)} %bitcast.27, f32[1,128]{1,0:T(1,128)} %bitcast.28, f32[512,128]{1,0:T(8,128)} %get-tuple-element.14.cos_o, ...), custom_call_target="tpu_custom_call" | custom-call | tf_op jit(solution)/shard_map/attention_backward/pallas_call | solution.py:199
  402.3 0.0 copy-start.6
  402.3 5.8 %all-to-all-start.2 = ((bf16[8,2,512,512]{3,2,1,0:T(8,128)(2,1)}), bf16[8,2,512,512]{3,2,1,0:T(8,128)(2,1)}, u32[]{:S(2)}, u32[]{:S(2)}) async-start(bf16[8,2,512,512]{3,2,1,0:T(8,128)(2,1)} %get-tuple-element.7), calls=%async_computation.2 | async-start | bytes 16777216 | tf_op jit(solution)/shard_map/all_to_all | solution.py:239
  408.2 0.0 copy-done.6
  408.2 98.0 %psum.7 = f32[2,128]{1,0:T(2,128)S(1)} all-reduce(f32[2,128]{1,0:T(2,128)S(1)} %pad_maximum_fusion.2), channel_id=1, replica_groups=mesh['dp'=2,'cp'=8] {'cp'}, use_global_device_ids=true, to_apply=%region_2.3 | all-reduce | flops 256 | bytes 2048 | tf_op jit(solution)/shard_map/psum | solution.py:244
  506.2 0.5 slice_bitcast_fusion.1
  506.7 0.0 all-to-all-done.2
  506.7 2.5 slice_bitcast_fusion
  509.2 4.0 fusion.5
  513.2 4.4 copy.17
  517.5 7.1 %reshape.66 = bf16[1024,16,128]{2,1,0:T(8,128)(2,1)} reshape(bf16[1024,8,256]{2,1,0:T(8,128)(2,1)} %copy.17) | data formatting | bytes 8388608 | tf_op jit(solution)/shard_map/reshape | solution.py:241
  524.6 6.3 %copy_bitcast_fusion = (bf16[1024,8,128]{2,1,0:T(8,128)(2,1)}, bf16[1024,8,128]{2,1,0:T(8,128)(2,1)}) fusion(bf16[8,1024,128]{2,1,0:T(8,128)(2,1)S(1)} %get-tuple-element.11, bf16[8,1024,128]{2,1,0:T(8,128)(2,1)} %get-tuple-element.12), kind=kLoop, calls=%fused_computation.4 | loop fusion | bytes 8388608 | tf_op jit(solution)/shard_map/transpose | solution.py:243
  (7 shorter events, 0.1 us)
Async XLA Ops:
  0.6 6.0 %copy-start.5 = (f32[1024,16]{0,1:T(8,128)S(1)}, f32[1024,16]{0,1:T(8,128)}, u32[]{:S(2)}) copy-start(f32[1024,16]{0,1:T(8,128)} %param.12) | copy-start | bytes 196612
  7.4 38.0 %all-to-all-start.1 = ((f32[8,2,8,512]{3,2,1,0:T(8,128)}), f32[8,2,8,512]{3,2,1,0:T(8,128)S(1)}, u32[]{:S(2)}, u32[]{:S(2)}) async-start(f32[8,2,8,512]{3,2,1,0:T(8,128)} %bitcast.3), calls=%async_computation.1 | async-start | bytes 524288 | tf_op jit(solution)/shard_map/all_to_all | solution.py:235
  20.5 5.1 copy-start.2
  25.7 1.6 copy-start.3
  36.0 3.4 copy-start
  36.0 4.1 copy-start.1
  45.4 0.7 copy-start.4
  46.1 144.1 %all-to-all-start = ((bf16[8,1024,768]{2,1,0:T(8,128)(2,1)}), bf16[8,1024,768]{2,1,0:T(8,128)(2,1)}, u32[]{:S(2)}, u32[]{:S(2)}) async-start(bf16[8,1024,768]{2,1,0:T(8,128)(2,1)} %maximum_bitcast_fusion), calls=%async_computation | async-start | bytes 25165824 | tf_op jit(solution)/shard_map/all_to_all | solution.py:234
  402.3 5.8 %copy-start.6 = (f32[16,128]{1,0:T(8,128)S(1)}, f32[16,128]{1,0:T(8,128)}, u32[]{:S(2)}) copy-start(f32[16,128]{1,0:T(8,128)} %get-tuple-element.8) | copy-start | bytes 24580
  402.3 104.4 %all-to-all-start.2 = ((bf16[8,2,512,512]{3,2,1,0:T(8,128)(2,1)}), bf16[8,2,512,512]{3,2,1,0:T(8,128)(2,1)}, u32[]{:S(2)}, u32[]{:S(2)}) async-start(bf16[8,2,512,512]{3,2,1,0:T(8,128)(2,1)} %get-tuple-element.7), calls=%async_computation.2 | async-start | bytes 16777216 | tf_op jit(solution)/shard_map/all_to_all | solution.py:239

commit v2 on v1

--- a/solution.py
+++ b/solution.py
@@ -55,7 +55,7 @@
     return hi, mid, x - hi - mid
 
 
-def prep_chunk(c, raw, ld, qw, kw, tabs, qr, qt, dot_, ext):
+def prep_chunk(c, src, half, raw, ld, qw, kw, tabs, qr, qt, dot_, ext):
     cos_t, sin_s = chunk_angles(c, *tabs)
     rows = raw.shape[1]
     for h in range(2):
@@ -65,7 +65,7 @@
         dot_[c, :, h * rows:(h + 1) * rows] = raw[c, :, 512 + h * 128:640 + h * 128].astype(F32).T.astype(BF16)
     y = norm_rope(raw[c, :, 256:384].astype(F32), kw[...], cos_t, sin_s)
     qr[c, :, 256:384] = y.astype(BF16)
-    vals = ld[c]
+    vals = ld[src, half]
     parts = []
     for t in range(4):
         parts.extend(split3(vals[t:t + 1] * (1.0 / SM_SCALE if t < 2 else 1.0)))
@@ -128,67 +128,190 @@
     raw[c, :, 384:512] = dvt[c].T.astype(BF16)
 
 
-def attn_kernel(slab, ld_in, qw, kw, cos_o, sin_o, cos_c, sin_c, out, dw,
-                raw, ld, qr, qt, dot_, ext, dq, dkt, dvt, sems):
+MESH = pl.DeviceIdType.MESH
+EARLY = 3
+
+
+def partner(me, step):
+    total = 0
+    for bit in (1, 2, 4):
+        a, b = (me // bit) % 2, (step // bit) % 2
+        total = total + bit * (a + b - 2 * a * b)
+    return total
+
+
+def visit_order(u):
+    return u + 2 * ((u // 4) % 2) * (1 - 2 * ((u // 2) % 2))
+
+
+def attn_kernel(slab, ld_in, qw, kw, cos_o, sin_o, cos_c, sin_c, out, dw_out,
+                raw, ld, qr, qt, dot_, ext, dq, dkt, dvt, dw, dw_all,
+                send_in, recv_in, send_ld, recv_ld, send_out, recv_out, send_dw, recv_dw, own_sem):
     n_chunks = raw.shape[0]
-    half = n_chunks // 2
+    n_dev = n_chunks // 2
+    me = lax.axis_index('cp')
     tabs = (cos_o, sin_o, cos_c, sin_c)
-
-    def slot(c):
-        dev = jnp.minimum(c, n_chunks - 1 - c)
-        return dev, (c >= half).astype(jnp.int32)
-
-    def load(c, start):
-        dev, part = slot(c)
-        one = pltpu.make_async_copy(slab.at[dev, part], raw.at[c], sems.at[c, 0])
-        two = pltpu.make_async_copy(ld_in.at[dev, part], ld.at[c], sems.at[c, 1])
-        if start:
-            one.start()
-            two.start()
-        else:
-            one.wait()
-            two.wait()
-
-    lax.fori_loop(0, n_chunks, lambda c, _: (load(c, True), 0)[1], 0)
+    block = functools.partial(block_grads, raw=raw, qr=qr, qt=qt, dot_=dot_, ext=ext, dq=dq, dkt=dkt, dvt=dvt)
+
+    def chunk_of(dev, half):
+        return dev + half * (n_chunks - 1 - 2 * dev)
+
+    def source(u):
+        return partner(me, visit_order(u))
+
+    def in_copy(half, dest, src):
+        return pltpu.make_async_remote_copy(
+            src_ref=slab.at[dest, half], dst_ref=raw.at[chunk_of(src, half)],
+            send_sem=send_in.at[dest, half], recv_sem=recv_in.at[src, half],
+            device_id={'cp': dest}, device_id_type=MESH)
+
+    def ld_copy(dest, src):
+        return pltpu.make_async_remote_copy(
+            src_ref=ld_in.at[dest], dst_ref=ld.at[src],
+            send_sem=send_ld.at[dest], recv_sem=recv_ld.at[src],
+            device_id={'cp': dest}, device_id_type=MESH)
+
+    def out_parts(part, half, chunk, src):
+        cols = (pl.ds(0, 256), pl.ds(256, 256), pl.ds(0, 512))[part]
+        return raw.at[chunk, :, cols], out.at[src, half, :, cols]
+
+    def out_copy(part, half, dest, src, chunk):
+        a, b = out_parts(part, half, chunk, src)
+        return pltpu.make_async_remote_copy(
+            src_ref=a, dst_ref=b, send_sem=send_out.at[dest, part], recv_sem=recv_out.at[src, part],
+            device_id={'cp': dest}, device_id_type=MESH)
+
+    def own_out(part, half):
+        a, b = out_parts(part, half, chunk_of(me, half), me)
+        return pltpu.make_async_copy(a, b, own_sem.at[3 + part])
+
+    def dw_copy(dest, src):
+        return pltpu.make_async_remote_copy(
+            src_ref=dw, dst_ref=dw_all.at[src], send_sem=send_dw.at[dest], recv_sem=recv_dw.at[src],
+            device_id={'cp': dest}, device_id_type=MESH)
+
+    def loop(lo, hi, body):
+        lax.fori_loop(lo, hi, lambda u, _: (body(u), 0)[1], 0)
+
+    own = [pltpu.make_async_copy(slab.at[me, h], raw.at[chunk_of(me, h)], own_sem.at[h]) for h in range(2)]
+    own.append(pltpu.make_async_copy(ld_in.at[me], ld.at[me], own_sem.at[2]))
+    for copy in own:
+        copy.start()
+
+    barrier = pltpu.get_barrier_semaphore()
+    loop(1, n_dev, lambda u: pl.semaphore_signal(barrier, inc=1, device_id={'cp': source(u)}, device_id_type=MESH))
+    pl.semaphore_wait(barrier, n_dev - 1)
+
+    loop(1, n_dev, lambda u: ld_copy(source(u), me).start())
+    for half in range(2):
+        loop(1, n_dev, lambda u, half=half: in_copy(half, source(u), me).start())
+
     dw[...] = jnp.zeros_like(dw)
     dq[...] = jnp.zeros_like(dq)
     dkt[...] = jnp.zeros_like(dkt)
     dvt[...] = jnp.zeros_like(dvt)
-
-    def prep(c, _):
-        load(c, False)
-        prep_chunk(c, raw, ld, qw, kw, tabs, qr, qt, dot_, ext)
-        return 0
-
-    lax.fori_loop(0, n_chunks, prep, 0)
-
-    def column(j, _):
-        block_grads(j, j, True, raw, qr, qt, dot_, ext, dq, dkt, dvt)
-
-        def row(i, _):
-            block_grads(i, j, False, raw, qr, qt, dot_, ext, dq, dkt, dvt)
-            return 0
-
-        lax.fori_loop(j + 1, n_chunks, row, 0)
-        return 0
-
-    lax.fori_loop(0, n_chunks, column, 0)
-
-    def finish(c, _):
-        finish_q(c, raw, qw, tabs, dq, dw)
-        finish_k(c, raw, kw, tabs, dkt, dvt, dw)
-        dev, part = slot(c)
-        pltpu.make_async_copy(raw.at[c, :, 0:512], out.at[dev, part], sems.at[c, 0]).start()
-        return 0
-
-    lax.fori_loop(0, n_chunks, finish, 0)
-
-    def drain(c, _):
-        dev, part = slot(c)
-        pltpu.make_async_copy(raw.at[c, :, 0:512], out.at[dev, part], sems.at[c, 0]).wait()
-        return 0
-
-    lax.fori_loop(0, n_chunks, drain, 0)
+    for copy in own:
+        copy.wait()
+
+    def arrive(u, half):
+        src = source(u)
+
+        @pl.when(u > 0)
+        def _():
+            in_copy(half, me, src).wait_recv()
+            if half == 0:
+                ld_copy(me, src).wait_recv()
+
+        prep_chunk(chunk_of(src, half), src, half, raw, ld, qw, kw, tabs, qr, qt, dot_, ext)
+
+    def send(u, part, half):
+        dest = source(u)
+
+        @pl.when(u > 0)
+        def _():
+            out_copy(part, half, dest, me, chunk_of(dest, half)).start()
+
+        @pl.when(u == 0)
+        def _():
+            own_out(part, half).start()
+
+    def pair(a, b):
+        block(jnp.maximum(a, b), jnp.minimum(a, b), False)
+
+    def diagonal(a):
+        block(a, a, True)
+
+    def low_round(u):
+        arrive(u, 0)
+        a = source(u)
+        loop(0, u, lambda w: pair(a, source(w)))
+        diagonal(a)
+
+    loop(0, n_dev, low_round)
+
+    def low_queries(u):
+        finish_q(source(u), raw, qw, tabs, dq, dw)
+        send(u, 0, 0)
+
+    loop(0, n_dev, low_queries)
+
+    def high_round(u):
+        arrive(u, 1)
+        a = chunk_of(source(u), 1)
+
+        def against(w):
+            half = w // n_dev
+            pair(a, chunk_of(source(w - half * n_dev), half))
+
+        loop(0, n_dev + u, against)
+        diagonal(a)
+
+    loop(0, EARLY, high_round)
+    loop(EARLY, n_dev, lambda u: arrive(u, 1))
+
+    def low_column(u):
+        j = source(u)
+        loop(EARLY, n_dev, lambda w: block(chunk_of(source(w), 1), j, False))
+        finish_k(j, raw, kw, tabs, dkt, dvt, dw)
+        send(u, 1, 0)
+
+    loop(0, n_dev, low_column)
+
+    def high_finish(u):
+        a = chunk_of(source(u), 1)
+        loop(jnp.maximum(u + 1, EARLY), n_dev, lambda w: pair(a, chunk_of(source(w), 1)))
+
+        @pl.when(u >= EARLY)
+        def _():
+            diagonal(a)
+
+        finish_q(a, raw, qw, tabs, dq, dw)
+        finish_k(a, raw, kw, tabs, dkt, dvt, dw)
+        send(u, 2, 1)
+
+    loop(0, n_dev, high_finish)
+
+    loop(1, n_dev, lambda u: dw_copy(source(u), me).start())
+    dw_all[me] = dw[...]
+
+    def settle(u):
+        src = source(u)
+        ld_copy(src, me).wait_send()
+        for half in range(2):
+            in_copy(half, src, me).wait_send()
+        for part in range(3):
+            out_copy(part, part // 2, src, me, chunk_of(src, part // 2)).wait_send()
+            out_copy(part, part // 2, me, src, chunk_of(me, part // 2)).wait_recv()
+        dw_copy(src, me).wait_send()
+        dw_copy(me, src).wait_recv()
+
+    loop(1, n_dev, settle)
+    for part in range(3):
+        own_out(part, part // 2).wait()
+    total = dw_all[0]
+    for src in range(1, n_dev):
+        total = total + dw_all[src]
+    dw_out[...] = total
 
 
 def run_attention(slab, ld, q_norm, k_norm, tabs):
@@ -196,6 +319,7 @@
     n_chunks = 2 * n_dev
     any_spec = pl.BlockSpec(memory_space=pl.ANY)
     vmem_spec = pl.BlockSpec(memory_space=pltpu.VMEM)
+    dma = pltpu.SemaphoreType.DMA
     return pl.pallas_call(
         attn_kernel,
         out_shape=(jax.ShapeDtypeStruct((n_dev, 2, rows, 512), BF16), jax.ShapeDtypeStruct((16, HEAD_DIM), F32)),
@@ -203,7 +327,7 @@
         out_specs=(any_spec, vmem_spec),
         scratch_shapes=[
             pltpu.VMEM((n_chunks, rows, 768), BF16),
-            pltpu.VMEM((n_chunks, 8, rows), F32),
+            pltpu.VMEM((n_dev, 2, 8, rows), F32),
             pltpu.VMEM((n_chunks, rows, 384), BF16),
             pltpu.VMEM((n_chunks, HEAD_DIM, 2 * rows), BF16),
             pltpu.VMEM((n_chunks, HEAD_DIM, 2 * rows), BF16),
@@ -211,11 +335,89 @@
             pltpu.VMEM((n_chunks, rows, 256), F32),
             pltpu.VMEM((n_chunks, HEAD_DIM, rows), F32),
             pltpu.VMEM((n_chunks, HEAD_DIM, rows), F32),
-            pltpu.SemaphoreType.DMA((n_chunks, 2)),
+            pltpu.VMEM((16, HEAD_DIM), F32),
+            pltpu.VMEM((n_dev, 16, HEAD_DIM), F32),
+            dma((n_dev, 2)), dma((n_dev, 2)), dma((n_dev,)), dma((n_dev,)),
+            dma((n_dev, 3)), dma((n_dev, 3)), dma((n_dev,)), dma((n_dev,)), dma((6,)),
         ],
-        compiler_params=pltpu.CompilerParams(vmem_limit_bytes=67043328),
+        compiler_params=pltpu.CompilerParams(vmem_limit_bytes=67043328, collective_id=0, has_side_effects=True),
         name='attention_backward',
     )(slab, ld, q_norm, k_norm, *tabs)
+
+
+def pack_kernel(q, k, v, o, lse, do, slab, ld, wide):
+    rows, heads = q.shape[0], q.shape[1]
+    groups = k.shape[1]
+
+    def scatter(x, n_heads, col):
+        per = n_heads // groups
+        wide[0:rows * n_heads, :] = x[...].reshape(rows * n_heads, HEAD_DIM).astype(F32)
+        for h in range(n_heads):
+            first = col + (h % per) * HEAD_DIM
+            slab[h // per, :, first:first + HEAD_DIM] = wide[pl.ds(h, rows, stride=n_heads), :].astype(BF16)
+
+    scatter(q, heads, 0)
+    scatter(k, groups, 256)
+    scatter(v, groups, 384)
+    scatter(do, heads, 512)
+    lse_t = lse[...].T
+    delta_t = jnp.sum(do[...].astype(F32) * o[...].astype(F32), axis=-1).T
+    for g in range(groups):
+        ld[g, 0] = jnp.concatenate([lse_t[2 * g:2 * g + 2], delta_t[2 * g:2 * g + 2], jnp.zeros((4, rows), F32)], axis=0)
+
+
+def pack_inputs(q, k, v, o, lse, do):
+    local_rows, heads, _ = q.shape
+    groups = k.shape[1]
+    blk = min(128, local_rows // 2)
+    per_half = local_rows // 2 // blk
+    big = pl.BlockSpec((blk, heads, HEAD_DIM), lambda i: (i, 0, 0))
+    small = pl.BlockSpec((blk, groups, HEAD_DIM), lambda i: (i, 0, 0))
+    return pl.pallas_call(
+        pack_kernel,
+        grid=(local_rows // blk,),
+        in_specs=[big, small, small, big, pl.BlockSpec((blk, heads), lambda i: (i, 0)), big],
+        out_specs=(pl.BlockSpec((groups, blk, 768), lambda i: (0, i, 0)),
+                   pl.BlockSpec((groups, 1, 8, blk), lambda i: (0, i // per_half, 0, i % per_half))),
+        out_shape=(jax.ShapeDtypeStruct((groups, local_rows, 768), BF16),
+                   jax.ShapeDtypeStruct((groups, 2, 8, local_rows // 2), F32)),
+        scratch_shapes=[pltpu.VMEM((blk * heads, HEAD_DIM), F32)],
+        name='pack_inputs',
+    )(q, k, v, o, lse, do)
+
+
+def unpack_kernel(out, dq, dk, dv, wide):
+    rows, heads = dq.shape[0], dq.shape[1]
+    groups = dk.shape[1]
+
+    def gather(dst, n_heads, col):
+        per = n_heads // groups
+        for h in range(n_heads):
+            first = col + (h % per) * HEAD_DIM
+            wide[pl.ds(h, rows, stride=n_heads), :] = out[h // per, :, first:first + HEAD_DIM].astype(F32)
+        dst[...] = wide[0:rows * n_heads, :].astype(BF16).reshape(rows, n_heads, HEAD_DIM)
+
+    gather(dq, heads, 0)
+    gather(dk, groups, 256)
+    gather(dv, groups, 384)
+
+
+def unpack_outputs(out, heads):
+    groups, local_rows, _ = out.shape
+    blk = min(128, local_rows // 2)
+    big = pl.BlockSpec((blk, heads, HEAD_DIM), lambda i: (i, 0, 0))
+    small = pl.BlockSpec((blk, groups, HEAD_DIM), lambda i: (i, 0, 0))
+    return pl.pallas_call(
+        unpack_kernel,
+        grid=(local_rows // blk,),
+        in_specs=[pl.BlockSpec((groups, blk, 512), lambda i: (0, i, 0))],
+        out_specs=(big, small, small),
+        out_shape=(jax.ShapeDtypeStruct((local_rows, heads, HEAD_DIM), BF16),
+                   jax.ShapeDtypeStruct((local_rows, groups, HEAD_DIM), BF16),
+                   jax.ShapeDtypeStruct((local_rows, groups, HEAD_DIM), BF16)),
+        scratch_shapes=[pltpu.VMEM((blk * heads, HEAD_DIM), F32)],
+        name='unpack_outputs',
+    )(out)
 
 
 def solution(mesh):
@@ -224,25 +426,11 @@
     def local_grads(q_raw, k_raw, v_proj, out_fwd, lse_fwd, d_out, q_norm, k_norm):
         local_rows, num_heads = q_raw.shape[0], q_raw.shape[1]
         rows = local_rows // 2
-        kv_heads = k_raw.shape[1]
-        by_group = lambda a: a.reshape(local_rows, kv_heads, -1)
-        slab = jnp.concatenate([by_group(q_raw), by_group(k_raw), by_group(v_proj), by_group(d_out)], axis=-1)
-        slab = slab.transpose(1, 0, 2)
-        delta = jnp.einsum('thd,thd->th', d_out, out_fwd, preferred_element_type=F32)
-        ld = jnp.concatenate([lse_fwd.reshape(local_rows, kv_heads, 2), delta.reshape(local_rows, kv_heads, 2)], axis=-1)
-        ld = jnp.pad(ld, ((0, 0), (0, 0), (0, 4))).reshape(2, rows, kv_heads, 8).transpose(2, 0, 3, 1)
-        slab = lax.all_to_all(slab, 'cp', 0, 0)
-        ld = lax.all_to_all(ld, 'cp', 0, 0)
-        slab = slab.reshape(cp_size, 2, rows, 768)
         tabs = angle_tables(jnp.arange(rows)) + angle_tables(jnp.arange(2 * cp_size) * rows)
-        out, dw = run_attention(slab, ld, q_norm.reshape(1, -1), k_norm.reshape(1, -1), tabs)
-        out = lax.all_to_all(out, 'cp', 0, 0)
-        out = out.reshape(kv_heads, local_rows, 512)
-        dq_raw = out[..., :256].transpose(1, 0, 2).reshape(local_rows, num_heads, HEAD_DIM)
-        dk_raw = out[..., 256:384].transpose(1, 0, 2)
-        dv = out[..., 384:].transpose(1, 0, 2)
-        dw = lax.psum(jnp.stack([dw[:8].sum(0), dw[8:].sum(0)]), 'cp')
-        return dq_raw, dk_raw, dv, dw[0], dw[1]
+        slab, ld = pack_inputs(q_raw, k_raw, v_proj, out_fwd, lse_fwd, d_out)
+        out, dw = run_attention(slab.reshape(cp_size, 2, rows, 768), ld, q_norm.reshape(1, -1), k_norm.reshape(1, -1), tabs)
+        dq_raw, dk_raw, dv = unpack_outputs(out.reshape(cp_size, local_rows, 512), num_heads)
+        return dq_raw, dk_raw, dv, dw[:8].sum(0), dw[8:].sum(0)
 
     row_spec = P(('dp', 'cp'))
     in_specs = (row_spec, row_spec, row_spec, row_spec, row_spec, row_spec, P(), P())

time: 533 us -> 326 us (0.61)
  waiting for transfers between devices: 136 us -> 0 us
  Pallas kernels: 212 us -> 320 us
  blocking collectives: 98 us -> 0 us
  local copies, waits for them, and re-layouts: 52.3 us -> 1.84 us
  starting transfers between devices: 17.4 us -> 0 us
  other arithmetic: 14.6 us -> 3.28 us
    all_to_all x3 -> x0, waiting for transfers between devices: 136 us -> none  [the longest x1 136 us: local_grads(): slab = lax.all_to_all(slab, 'cp', 0, 0)]
    psum x1 -> x0, blocking collectives: 98 us -> none  [local_grads(): dw = lax.psum(jnp.stack([dw[:8].sum(0), dw[8:].sum(0)]), 'cp')]
    pallas_call x1, Pallas kernels: 212 us -> 292 us  [run_attention(): pl.pallas_call(attn_kernel, out_shape=(jax.ShapeDtypeStruct((n_dev, 2, ro...]
    reshape x7 -> x0, local copies, waits for them, and re-layouts: 29.6 us -> none  [the longest x4 22.5 us: local_grads(): by_group = lambda a: a.reshape(local_rows, kv_heads, -1)]
    pallas_call x0 -> x2, Pallas kernels: none -> 28.1 us  [the longest x1 17 us: pack_inputs(): pl.pallas_call(pack_kernel, grid=(local_rows // blk,), in_specs=[big, sma...]
    all_to_all x3 -> x0, starting transfers between devices: 17.4 us -> none  [the longest x1 6.02 us: local_grads(): ld = lax.all_to_all(ld, 'cp', 0, 0)]
    transpose x3 -> x0, local copies, waits for them, and re-layouts: 13.1 us -> none  [the longest x2 6.81 us: local_grads(): out[..., :256].transpose(1, 0, 2).reshape(local_rows, num_heads, HEAD_DIM)]
    unnamed x1 -> x0, other arithmetic: 5.73 us -> none
  transfers between devices with their start and end apart: 3 -> 0, of which waited for: 1 -> 0; matrix products, arithmetic and copies ran while one was open for 6% -> 0% of each run, Pallas kernels for 0% -> 0%
where the time goes in v2:
time: 326 us
  Pallas kernels  320 us (98%)
  other arithmetic  3.28 us (1%)
    pallas_call x1, Pallas kernels, run_attention(): pl.pallas_call(attn_kernel, out_shape=(jax.ShapeDtypeStruct((n_dev, 2, ro...  292 us
    pallas_call x1, Pallas kernels, pack_inputs(): pl.pallas_call(pack_kernel, grid=(local_rows // blk,), in_specs=[big, sma...  17 us
    pallas_call x1, Pallas kernels, unpack_outputs(): pl.pallas_call(unpack_kernel, grid=(local_rows // blk,), in_specs=[pl.Blo...  11.1 us

profile of v2, /device:TPU:113, one launch (start us, length us, event | category | flops | bytes accessed | tf_op | source)
XLA Modules:
  0.0 325.8 jit_solution(13246086260269006224)
XLA Ops:
  0.7 0.1 broadcast_multiply_fusion.1
  0.7 0.7 fusion.2
  1.5 0.1 broadcast_multiply_fusion
  1.6 1.8 fusion
  3.4 1.8 copy.13.lse
  5.2 17.0 %pack_inputs.1 = (bf16[8,1024,768]{2,1,0:T(8,128)(2,1)}, f32[8,2,8,512]{3,2,1,0:T(8,128)}) custom-call(bf16[1024,16,128]{2,1,0:T(8,128)(2,1)} %q.1, bf16[1024,8,128]{2,1,0:T(8,128)(2,1)} %k.1, bf16[1024,8,128]{2,1,0:T(8,128)(2,1)} %v.1, bf16[1024,16,128]{2,1,0:T(8,128)(2,1)} %o.1, f32[1024,16]{1,0:T(8,128)} %copy.13.lse, bf16[1024,16,128]{2,1,0:T(8,128)(2,1)} %do.1), custom_call_target="tpu_custom_call" | custom-call | tf_op jit(solution)/shard_map/pack_inputs/pallas_call | solution.py:376
  22.3 291.9 %attention_backward.1 = (bf16[8,2,512,512]{3,2,1,0:T(8,128)(2,1)}, f32[16,128]{1,0:T(8,128)}) custom-call(bf16[8,2,512,768]{3,2,1,0:T(8,128)(2,1)} %bitcast.4, f32[8,2,8,512]{3,2,1,0:T(8,128)} %get-tuple-element.13.ld_in, f32[1,128]{1,0:T(1,128)} %bitcast.6, f32[1,128]{1,0:T(1,128)} %bitcast.7, f32[512,128]{1,0:T(8,128)} %get-tuple-element.22.cos_o, ...), custom_call_target="tpu_custom_call" | custom-call | tf_op jit(solution)/shard_map/attention_backward/pallas_call | solution.py:323
  314.2 0.0 copy-start
  314.2 11.1 %unpack_outputs.1 = (bf16[1024,16,128]{2,1,0:T(8,128)(2,1)}, bf16[1024,8,128]{2,1,0:T(8,128)(2,1)}, bf16[1024,8,128]{2,1,0:T(8,128)(2,1)}) custom-call(bf16[8,1024,512]{2,1,0:T(8,128)(2,1)} %bitcast.5), custom_call_target="tpu_custom_call" | custom-call | tf_op jit(solution)/shard_map/unpack_outputs/pallas_call | solution.py:410
  325.2 0.0 copy-done
  325.2 0.5 slice_reduce_fusion
  (3 shorter events, 0.0 us)
Async XLA Ops:
  314.2 11.1 %copy-start = (f32[16,128]{1,0:T(8,128)S(1)}, f32[16,128]{1,0:T(8,128)}, u32[]{:S(2)}) copy-start(f32[16,128]{1,0:T(8,128)} %get-tuple-element.18) | copy-start | bytes 24580

commit v3 on v2

--- a/solution.py
+++ b/solution.py
@@ -55,22 +55,22 @@
     return hi, mid, x - hi - mid
 
 
-def prep_chunk(c, src, half, raw, ld, qw, kw, tabs, qr, qt, dot_, ext):
+def prep_chunk(c, src, half, raw, ld, qw, kw, tabs, qr, qt, dot_, kt, ext):
     cos_t, sin_s = chunk_angles(c, *tabs)
     rows = raw.shape[1]
     for h in range(2):
         y = norm_rope(raw[c, :, h * 128:(h + 1) * 128].astype(F32), qw[...], cos_t, sin_s)
         qr[c, :, h * 128:(h + 1) * 128] = y.astype(BF16)
-        qt[c, :, h * rows:(h + 1) * rows] = y.T.astype(BF16)
-        dot_[c, :, h * rows:(h + 1) * rows] = raw[c, :, 512 + h * 128:640 + h * 128].astype(F32).T.astype(BF16)
+        qt[c, :, h * rows:(h + 1) * rows] = y.astype(BF16).T
+        dot_[c, :, h * rows:(h + 1) * rows] = raw[c, :, 512 + h * 128:640 + h * 128].T
     y = norm_rope(raw[c, :, 256:384].astype(F32), kw[...], cos_t, sin_s)
     qr[c, :, 256:384] = y.astype(BF16)
+    kt[c] = y.astype(BF16).T
     vals = ld[src, half]
-    parts = []
-    for t in range(4):
-        parts.extend(split3(vals[t:t + 1] * (1.0 / SM_SCALE if t < 2 else 1.0)))
-    parts.append(jnp.zeros((HEAD_DIM - 12, rows), F32))
-    ext[c] = jnp.concatenate(parts, axis=0).T.astype(BF16)
+    for h in range(2):
+        parts = list(split3(vals[h:h + 1] * (1.0 / SM_SCALE))) + list(split3(vals[2 + h:3 + h]))
+        parts.append(jnp.zeros((HEAD_DIM - 6, rows), F32))
+        ext[c, :, h * 128:(h + 1) * 128] = jnp.concatenate(parts, axis=0).astype(BF16).T
 
 
 def minus_one_lanes(rows, first):
@@ -86,36 +86,49 @@
     return lax.dot_general(a, b, (((1,), (0,)), ((), ())), preferred_element_type=F32)
 
 
-def block_grads(i, j, masked, raw, qr, qt, dot_, ext, dq, dkt, dvt):
+def tile_grads(i, j, q0, qn, kn, masked, raw, qr, qt, dot_, kt, ext, dqt, dkt, dvt):
     rows = raw.shape[1]
-    kb = qr[j, :, 256:384]
-    vb = raw[j, :, 384:512]
-    ex = ext[i]
-    probs, grads = [], []
+    ke = jnp.concatenate([qr[j, 0:kn, 256:384], minus_one_lanes(kn, 0)], axis=1)
+    ve = jnp.concatenate([raw[j, 0:kn, 384:512], minus_one_lanes(kn, 3)], axis=1)
+    span = slice(q0, q0 + qn)
+    ex = jnp.concatenate([ext[i, span, 0:128], ext[i, span, 128:256]], axis=0)
+    q_all = jnp.concatenate([qr[i, span, 0:128], qr[i, span, 128:256]], axis=0)
+    do_all = jnp.concatenate([raw[i, span, 512:640], raw[i, span, 640:768]], axis=0)
+    s = dot_t(jnp.concatenate([q_all, ex], axis=1), ke)
+    if masked:
+        r_id = lax.rem(lax.broadcasted_iota(jnp.int32, s.shape, 0), qn) + q0
+        c_id = lax.broadcasted_iota(jnp.int32, s.shape, 1)
+        s = jnp.where(r_id >= c_id, s, -jnp.inf)
+    p = jnp.exp(s * SM_SCALE)
+    ds = (p * dot_t(jnp.concatenate([do_all, ex], axis=1), ve)).astype(BF16)
+    spans = [slice(h * rows + q0, h * rows + q0 + qn) for h in range(2)]
+    both = lambda ref: jnp.concatenate([ref[i, :, cols] for cols in spans], axis=1)
+    dvt[j, :, 0:kn] += dot_n(both(dot_), p.astype(BF16))
+    dkt[j, :, 0:kn] += dot_n(both(qt), ds)
+    dq_part = dot_t(kt[j, :, 0:kn], ds)
     for h in range(2):
-        ke = jnp.concatenate([kb, minus_one_lanes(rows, 3 * h)], axis=1)
-        ve = jnp.concatenate([vb, minus_one_lanes(rows, 6 + 3 * h)], axis=1)
-        qe = jnp.concatenate([qr[i, :, h * 128:(h + 1) * 128], ex], axis=1)
-        de = jnp.concatenate([raw[i, :, 512 + h * 128:640 + h * 128], ex], axis=1)
-        s = dot_t(qe, ke)
-        if masked:
-            r_id = lax.broadcasted_iota(jnp.int32, s.shape, 0)
-            c_id = lax.broadcasted_iota(jnp.int32, s.shape, 1)
-            s = jnp.where(r_id >= c_id, s, -jnp.inf)
-        p = jnp.exp(s * SM_SCALE)
-        ds = (p * dot_t(de, ve)).astype(BF16)
-        probs.append(p.astype(BF16))
-        grads.append(ds)
-        dq[i, :, h * 128:(h + 1) * 128] += dot_n(ds, kb)
-    dvt[j] += dot_n(dot_[i], jnp.concatenate(probs, axis=0))
-    dkt[j] += dot_n(qt[i], jnp.concatenate(grads, axis=0))
-
-
-def finish_q(c, raw, qw, tabs, dq, dw):
+        dqt[i, :, spans[h]] += dq_part[:, h * qn:(h + 1) * qn]
+
+
+def block_grads(i, j, **refs):
+    rows = refs['raw'].shape[1]
+    for q0 in (0, rows // 2):
+        tile_grads(i, j, q0, rows // 2, rows, False, **refs)
+
+
+def diagonal_grads(i, **refs):
+    half = refs['raw'].shape[1] // 2
+    tile_grads(i, i, 0, half, half, True, **refs)
+    tile_grads(i, i, half, half, 2 * half, True, **refs)
+
+
+def finish_q(c, raw, qw, tabs, dqt, dw):
     cos_t, sin_s = chunk_angles(c, *tabs)
+    rows = raw.shape[1]
     for h in range(2):
         cols = slice(h * 128, (h + 1) * 128)
-        dx, part = norm_rope_grad(raw[c, :, cols].astype(F32), qw[...], cos_t, sin_s, dq[c, :, cols] * SM_SCALE)
+        grad = dqt[c, :, h * rows:(h + 1) * rows].T * SM_SCALE
+        dx, part = norm_rope_grad(raw[c, :, cols].astype(F32), qw[...], cos_t, sin_s, grad)
         raw[c, :, cols] = dx.astype(BF16)
         dw[0:8, :] += part
 
@@ -129,35 +142,36 @@
 
 
 MESH = pl.DeviceIdType.MESH
-EARLY = 3
+EARLY = 5
 
 
 def partner(me, step):
-    total = 0
+    total = me + step
     for bit in (1, 2, 4):
-        a, b = (me // bit) % 2, (step // bit) % 2
-        total = total + bit * (a + b - 2 * a * b)
+        total = total - 2 * bit * lax.rem(lax.div(me, bit), 2) * lax.rem(lax.div(step, bit), 2)
     return total
 
 
 def visit_order(u):
-    return u + 2 * ((u // 4) % 2) * (1 - 2 * ((u // 2) % 2))
+    return u + 2 * lax.div(u, 4) * (1 - 2 * lax.rem(lax.div(u, 2), 2))
 
 
 def attn_kernel(slab, ld_in, qw, kw, cos_o, sin_o, cos_c, sin_c, out, dw_out,
-                raw, ld, qr, qt, dot_, ext, dq, dkt, dvt, dw, dw_all,
+                raw, ld, qr, qt, dot_, kt, ext, dqt, dkt, dvt, dw, dw_all,
                 send_in, recv_in, send_ld, recv_ld, send_out, recv_out, send_dw, recv_dw, own_sem):
     n_chunks = raw.shape[0]
     n_dev = n_chunks // 2
     me = lax.axis_index('cp')
     tabs = (cos_o, sin_o, cos_c, sin_c)
-    block = functools.partial(block_grads, raw=raw, qr=qr, qt=qt, dot_=dot_, ext=ext, dq=dq, dkt=dkt, dvt=dvt)
+    refs = dict(raw=raw, qr=qr, qt=qt, dot_=dot_, kt=kt, ext=ext, dqt=dqt, dkt=dkt, dvt=dvt)
+    block = functools.partial(block_grads, **refs)
+    diagonal = functools.partial(diagonal_grads, **refs)
 
     def chunk_of(dev, half):
         return dev + half * (n_chunks - 1 - 2 * dev)
 
     def source(u):
-        return partner(me, visit_order(u))
+        return partner(me, visit_order(jnp.int32(u)))
 
     def in_copy(half, dest, src):
         return pltpu.make_async_remote_copy(
@@ -193,6 +207,19 @@
     def loop(lo, hi, body):
         lax.fori_loop(lo, hi, lambda u, _: (body(u), 0)[1], 0)
 
+    def loop_by_two(lo, hi, body):
+        count = hi - lo
+
+        def two(m):
+            body(lo + 2 * m)
+            body(lo + 2 * m + 1)
+
+        loop(0, count // 2, two)
+
+        @pl.when(count % 2 == 1)
+        def _():
+            body(hi - 1)
+
     own = [pltpu.make_async_copy(slab.at[me, h], raw.at[chunk_of(me, h)], own_sem.at[h]) for h in range(2)]
     own.append(pltpu.make_async_copy(ld_in.at[me], ld.at[me], own_sem.at[2]))
     for copy in own:
@@ -204,25 +231,30 @@
 
     loop(1, n_dev, lambda u: ld_copy(source(u), me).start())
     for half in range(2):
-        loop(1, n_dev, lambda u, half=half: in_copy(half, source(u), me).start())
+        in_copy(half, source(1), me).start()
+    for half in range(2):
+        loop(2, n_dev, lambda u, half=half: in_copy(half, source(u), me).start())
 
     dw[...] = jnp.zeros_like(dw)
-    dq[...] = jnp.zeros_like(dq)
+    dqt[...] = jnp.zeros_like(dqt)
     dkt[...] = jnp.zeros_like(dkt)
     dvt[...] = jnp.zeros_like(dvt)
     for copy in own:
         copy.wait()
 
-    def arrive(u, half):
-        src = source(u)
-
-        @pl.when(u > 0)
+    def arrive(t):
+        visit, half = stop(t)
+        src = source(visit)
+
+        @pl.when(visit > 0)
         def _():
             in_copy(half, me, src).wait_recv()
-            if half == 0:
-                ld_copy(me, src).wait_recv()
-
-        prep_chunk(chunk_of(src, half), src, half, raw, ld, qw, kw, tabs, qr, qt, dot_, ext)
+
+        @pl.when((visit > 0) & (half == 0))
+        def _():
+            ld_copy(me, src).wait_recv()
+
+        prep_chunk(chunk_of(src, half), src, half, raw, ld, qw, kw, tabs, qr, qt, dot_, kt, ext)
 
     def send(u, part, half):
         dest = source(u)
@@ -235,43 +267,42 @@
         def _():
             own_out(part, half).start()
 
+    def stop(t):
+        t = jnp.int32(t)
+        late = lax.div(t + 12, 16)
+        visit = (1 - late) * lax.rem(t, 2) + late * (2 + lax.rem(t + 2, 6))
+        half = (1 - late) * lax.div(t, 2) + late * (lax.div(t + 2, 6) - 1)
+        return visit, half
+
+    def chunk_at(t):
+        visit, half = stop(t)
+        return chunk_of(source(visit), half)
+
     def pair(a, b):
-        block(jnp.maximum(a, b), jnp.minimum(a, b), False)
-
-    def diagonal(a):
-        block(a, a, True)
-
-    def low_round(u):
-        arrive(u, 0)
-        a = source(u)
-        loop(0, u, lambda w: pair(a, source(w)))
+        block(jnp.maximum(a, b), jnp.minimum(a, b))
+
+    def row_round(t):
+        arrive(t)
+        a = chunk_at(t)
+        loop_by_two(0, t, lambda w: pair(a, chunk_at(w)))
         diagonal(a)
 
-    loop(0, n_dev, low_round)
+    n_low = n_dev + 2
+    n_row = n_low + EARLY - 2
+    loop(0, n_low, row_round)
 
     def low_queries(u):
-        finish_q(source(u), raw, qw, tabs, dq, dw)
+        finish_q(source(u), raw, qw, tabs, dqt, dw)
         send(u, 0, 0)
 
     loop(0, n_dev, low_queries)
-
-    def high_round(u):
-        arrive(u, 1)
-        a = chunk_of(source(u), 1)
-
-        def against(w):
-            half = w // n_dev
-            pair(a, chunk_of(source(w - half * n_dev), half))
-
-        loop(0, n_dev + u, against)
-        diagonal(a)
-
-    loop(0, EARLY, high_round)
-    loop(EARLY, n_dev, lambda u: arrive(u, 1))
+    loop(n_low, n_row, row_round)
+    loop(n_row, n_chunks, arrive)
 
     def low_column(u):
         j = source(u)
-        loop(EARLY, n_dev, lambda w: block(chunk_of(source(w), 1), j, False))
+        for w in range(n_row, n_chunks):
+            block(chunk_at(w), j)
         finish_k(j, raw, kw, tabs, dkt, dvt, dw)
         send(u, 1, 0)
 
@@ -279,13 +310,13 @@
 
     def high_finish(u):
         a = chunk_of(source(u), 1)
-        loop(jnp.maximum(u + 1, EARLY), n_dev, lambda w: pair(a, chunk_of(source(w), 1)))
+        loop_by_two(jnp.maximum(u + 1, EARLY), n_dev, lambda w: pair(a, chunk_of(source(w), 1)))
 
         @pl.when(u >= EARLY)
         def _():
             diagonal(a)
 
-        finish_q(a, raw, qw, tabs, dq, dw)
+        finish_q(a, raw, qw, tabs, dqt, dw)
         finish_k(a, raw, kw, tabs, dkt, dvt, dw)
         send(u, 2, 1)
 
@@ -331,8 +362,9 @@
             pltpu.VMEM((n_chunks, rows, 384), BF16),
             pltpu.VMEM((n_chunks, HEAD_DIM, 2 * rows), BF16),
             pltpu.VMEM((n_chunks, HEAD_DIM, 2 * rows), BF16),
-            pltpu.VMEM((n_chunks, rows, HEAD_DIM), BF16),
-            pltpu.VMEM((n_chunks, rows, 256), F32),
+            pltpu.VMEM((n_chunks, HEAD_DIM, rows), BF16),
+            pltpu.VMEM((n_chunks, rows, 256), BF16),
+            pltpu.VMEM((n_chunks, HEAD_DIM, 2 * rows), F32),
             pltpu.VMEM((n_chunks, HEAD_DIM, rows), F32),
             pltpu.VMEM((n_chunks, HEAD_DIM, rows), F32),
             pltpu.VMEM((16, HEAD_DIM), F32),

time: 326 us -> 313 us (0.960)
  Pallas kernels: 320 us -> 306 us
    pallas_call x1, Pallas kernels: 292 us -> 278 us  [run_attention(): pl.pallas_call(attn_kernel, out_shape=(jax.ShapeDtypeStruct((n_dev, 2, ro...]
where the time goes in v3:
time: 313 us; the launch traced here: 312 us
  Pallas kernels  306 us (98%)
  other arithmetic  3.28 us (1%)
    pallas_call x1, Pallas kernels, run_attention(): pl.pallas_call(attn_kernel, out_shape=(jax.ShapeDtypeStruct((n_dev, 2, ro...  278 us
    pallas_call x1, Pallas kernels, pack_inputs(): pl.pallas_call(pack_kernel, grid=(local_rows // blk,), in_specs=[big, sma...  17 us
    pallas_call x1, Pallas kernels, unpack_outputs(): pl.pallas_call(unpack_kernel, grid=(local_rows // blk,), in_specs=[pl.Blo...  11.1 us

profile of v3, /device:TPU:113, one launch (start us, length us, event | category | flops | bytes accessed | tf_op | source)
XLA Modules:
  0.0 312.2 jit_solution(1116086085208358356)
XLA Ops:
  0.7 0.1 broadcast_multiply_fusion.1
  0.7 0.7 fusion.2
  1.5 0.1 broadcast_multiply_fusion
  1.6 1.8 fusion
  3.4 1.8 copy.13.lse
  5.2 17.0 %pack_inputs.1 = (bf16[8,1024,768]{2,1,0:T(8,128)(2,1)}, f32[8,2,8,512]{3,2,1,0:T(8,128)}) custom-call(bf16[1024,16,128]{2,1,0:T(8,128)(2,1)} %q.1, bf16[1024,8,128]{2,1,0:T(8,128)(2,1)} %k.1, bf16[1024,8,128]{2,1,0:T(8,128)(2,1)} %v.1, bf16[1024,16,128]{2,1,0:T(8,128)(2,1)} %o.1, f32[1024,16]{1,0:T(8,128)} %copy.13.lse, bf16[1024,16,128]{2,1,0:T(8,128)(2,1)} %do.1), custom_call_target="tpu_custom_call" | custom-call | tf_op jit(solution)/shard_map/pack_inputs/pallas_call | solution.py:408
  22.3 278.3 %attention_backward.1 = (bf16[8,2,512,512]{3,2,1,0:T(8,128)(2,1)}, f32[16,128]{1,0:T(8,128)}) custom-call(bf16[8,2,512,768]{3,2,1,0:T(8,128)(2,1)} %bitcast.4, f32[8,2,8,512]{3,2,1,0:T(8,128)} %get-tuple-element.13.ld_in, f32[1,128]{1,0:T(1,128)} %bitcast.6, f32[1,128]{1,0:T(1,128)} %bitcast.7, f32[512,128]{1,0:T(8,128)} %get-tuple-element.22.cos_o, ...), custom_call_target="tpu_custom_call" | custom-call | tf_op jit(solution)/shard_map/attention_backward/pallas_call | solution.py:354
  300.6 0.0 copy-start
  300.6 11.1 %unpack_outputs.1 = (bf16[1024,16,128]{2,1,0:T(8,128)(2,1)}, bf16[1024,8,128]{2,1,0:T(8,128)(2,1)}, bf16[1024,8,128]{2,1,0:T(8,128)(2,1)}) custom-call(bf16[8,1024,512]{2,1,0:T(8,128)(2,1)} %bitcast.5), custom_call_target="tpu_custom_call" | custom-call | tf_op jit(solution)/shard_map/unpack_outputs/pallas_call | solution.py:442
  311.6 0.0 copy-done
  311.6 0.5 slice_reduce_fusion
  (3 shorter events, 0.0 us)
Async XLA Ops:
  300.6 11.1 %copy-start = (f32[16,128]{1,0:T(8,128)S(1)}, f32[16,128]{1,0:T(8,128)}, u32[]{:S(2)}) copy-start(f32[16,128]{1,0:T(8,128)} %get-tuple-element.18) | copy-start | bytes 24580

commit v4 on v3

--- a/solution.py
+++ b/solution.py
@@ -232,8 +232,7 @@
     loop(1, n_dev, lambda u: ld_copy(source(u), me).start())
     for half in range(2):
         in_copy(half, source(1), me).start()
-    for half in range(2):
-        loop(2, n_dev, lambda u, half=half: in_copy(half, source(u), me).start())
+    loop(2, n_dev, lambda u: in_copy(0, source(u), me).start())
 
     dw[...] = jnp.zeros_like(dw)
     dqt[...] = jnp.zeros_like(dqt)
@@ -254,6 +253,11 @@
         def _():
             ld_copy(me, src).wait_recv()
 
+        @pl.when((t >= 4) & (t < 7))
+        def _():
+            for step in range(2):
+                in_copy(1, source(2 * t - 6 + step), me).start()
+
         prep_chunk(chunk_of(src, half), src, half, raw, ld, qw, kw, tabs, qr, qt, dot_, kt, ext)
 
     def send(u, part, half):
@@ -290,14 +294,14 @@
     n_low = n_dev + 2
     n_row = n_low + EARLY - 2
     loop(0, n_low, row_round)
+    loop(n_low, n_row, row_round)
+    loop(n_row, n_chunks, arrive)
 
     def low_queries(u):
         finish_q(source(u), raw, qw, tabs, dqt, dw)
         send(u, 0, 0)
 
     loop(0, n_dev, low_queries)
-    loop(n_low, n_row, row_round)
-    loop(n_row, n_chunks, arrive)
 
     def low_column(u):
         j = source(u)

time: 313 us -> 312 us (level)
  no operation moved by 1% of the time
where the time goes in v4:
time: 312 us
  Pallas kernels  306 us (98%)
  other arithmetic  3.28 us (1%)
    pallas_call x1, Pallas kernels, run_attention(): pl.pallas_call(attn_kernel, out_shape=(jax.ShapeDtypeStruct((n_dev, 2, ro...  278 us
    pallas_call x1, Pallas kernels, pack_inputs(): pl.pallas_call(pack_kernel, grid=(local_rows // blk,), in_specs=[big, sma...  17 us
    pallas_call x1, Pallas kernels, unpack_outputs(): pl.pallas_call(unpack_kernel, grid=(local_rows // blk,), in_specs=[pl.Blo...  11.1 us

profile of v4, /device:TPU:113, one launch (start us, length us, event | category | flops | bytes accessed | tf_op | source)
XLA Modules:
  0.0 311.6 jit_solution(17922262852777564888)
XLA Ops:
  0.7 0.1 broadcast_multiply_fusion.1
  0.7 0.7 fusion.2
  1.5 0.1 broadcast_multiply_fusion
  1.6 1.8 fusion
  3.4 1.8 copy.13.lse
  5.2 17.0 %pack_inputs.1 = (bf16[8,1024,768]{2,1,0:T(8,128)(2,1)}, f32[8,2,8,512]{3,2,1,0:T(8,128)}) custom-call(bf16[1024,16,128]{2,1,0:T(8,128)(2,1)} %q.1, bf16[1024,8,128]{2,1,0:T(8,128)(2,1)} %k.1, bf16[1024,8,128]{2,1,0:T(8,128)(2,1)} %v.1, bf16[1024,16,128]{2,1,0:T(8,128)(2,1)} %o.1, f32[1024,16]{1,0:T(8,128)} %copy.13.lse, bf16[1024,16,128]{2,1,0:T(8,128)(2,1)} %do.1), custom_call_target="tpu_custom_call" | custom-call | tf_op jit(solution)/shard_map/pack_inputs/pallas_call | solution.py:412
  22.3 277.7 %attention_backward.1 = (bf16[8,2,512,512]{3,2,1,0:T(8,128)(2,1)}, f32[16,128]{1,0:T(8,128)}) custom-call(bf16[8,2,512,768]{3,2,1,0:T(8,128)(2,1)} %bitcast.4, f32[8,2,8,512]{3,2,1,0:T(8,128)} %get-tuple-element.13.ld_in, f32[1,128]{1,0:T(1,128)} %bitcast.6, f32[1,128]{1,0:T(1,128)} %bitcast.7, f32[512,128]{1,0:T(8,128)} %get-tuple-element.22.cos_o, ...), custom_call_target="tpu_custom_call" | custom-call | tf_op jit(solution)/shard_map/attention_backward/pallas_call | solution.py:358
  300.0 0.0 copy-start
  300.0 11.1 %unpack_outputs.1 = (bf16[1024,16,128]{2,1,0:T(8,128)(2,1)}, bf16[1024,8,128]{2,1,0:T(8,128)(2,1)}, bf16[1024,8,128]{2,1,0:T(8,128)(2,1)}) custom-call(bf16[8,1024,512]{2,1,0:T(8,128)(2,1)} %bitcast.5), custom_call_target="tpu_custom_call" | custom-call | tf_op jit(solution)/shard_map/unpack_outputs/pallas_call | solution.py:446
  311.0 0.0 copy-done
  311.0 0.5 slice_reduce_fusion
  (3 shorter events, 0.0 us)
Async XLA Ops:
  300.0 11.1 %copy-start = (f32[16,128]{1,0:T(8,128)S(1)}, f32[16,128]{1,0:T(8,128)}, u32[]{:S(2)}) copy-start(f32[16,128]{1,0:T(8,128)} %get-tuple-element.18) | copy-start | bytes 24580
